TPU v7x, 128 devices: a whole 4x4x4 slice. The times are simulated.
128 devices in a mesh: dp: 1, sp: 128 (over z, y, x, core).
Axes of the slice: x: 4, y: 4, z: 4, core: 2. Of those that a mesh axis runs over, the one named last changes fastest.
Arguments:
- pair_rep: float32 [768, 768, 128], P(('dp', 'sp'))
- w_qkvg_s: bfloat16 [128, 512], replicated
- w_bias_s: bfloat16 [4, 128], replicated
- w_out_s: bfloat16 [128, 128], replicated
- w_qkvg_e: bfloat16 [128, 512], replicated
- w_bias_e: bfloat16 [4, 128], replicated
- w_out_e: bfloat16 [128, 128], replicated
- w_one: bfloat16 [128, 512], replicated
- w_two: bfloat16 [512, 128], replicated
Outputs:
- output: float32 [768, 768, 128], P(('dp', 'sp'))
All inputs are finite; a program needn't handle non-finite values.
Results may differ from a plain program's by a relative error of at most 0.0108011.
Values are sent between devices in bfloat16 or wider.
A program may use at most 1 GiB of HBM per device.

v0:
```python
import jax
import jax.numpy as jnp
from jax import lax
from jax.sharding import PartitionSpec as P

LN_EPS = 1e-5
SCORE_CAP = 2 ** 23


def layer_norm(values):
    vals_f = values.astype(jnp.float32)
    mean_c = jnp.mean(vals_f, axis=-1, keepdims=True)
    centered = vals_f - mean_c
    variance = jnp.mean(centered * centered, axis=-1, keepdims=True)
    return (centered * lax.rsqrt(variance + LN_EPS)).astype(jnp.bfloat16)


def project(normed, w_qkvg, num_heads):
    channels = w_qkvg.shape[0]
    projected = jnp.dot(normed, w_qkvg, preferred_element_type=jnp.float32)
    split_shape = normed.shape[:-1] + (num_heads, channels // num_heads)
    queries = projected[..., :channels].astype(jnp.bfloat16).reshape(split_shape)
    key_vecs = projected[..., channels:2 * channels].astype(jnp.bfloat16).reshape(split_shape)
    val_vecs = projected[..., 2 * channels:3 * channels].astype(jnp.bfloat16).reshape(split_shape)
    gate_vals = jax.nn.sigmoid(projected[..., 3 * channels:]).reshape(split_shape)
    return queries, key_vecs, val_vecs, gate_vals


def attend(queries, key_vecs, val_vecs, gate_vals, bias_full, w_out, score_form, mix_form):
    head_dim = queries.shape[-1]
    scores = jnp.einsum(score_form, queries, key_vecs, preferred_element_type=jnp.float32)
    scores = scores * head_dim ** -0.5 + bias_full.astype(jnp.float32)
    attn_prob = jax.nn.softmax(scores, axis=-1).astype(jnp.bfloat16)
    attn_out = jnp.einsum(mix_form, attn_prob, val_vecs, preferred_element_type=jnp.float32)
    gated_out = (attn_out * gate_vals).astype(jnp.bfloat16)
    merged = gated_out.reshape(gated_out.shape[:-2] + (w_out.shape[0],))
    return jnp.dot(merged, w_out, preferred_element_type=jnp.float32)


def transition(resid_in, w_one, w_two):
    hidden = jax.nn.relu(jnp.dot(layer_norm(resid_in), w_one, preferred_element_type=jnp.float32))
    return jnp.dot(hidden.astype(jnp.bfloat16), w_two, preferred_element_type=jnp.float32)


def block_size(total_len, per_item):
    return max(candidate for candidate in range(1, total_len + 1) if total_len % candidate == 0 and (candidate == 1 or candidate * per_item <= SCORE_CAP))


def solution(mesh):
    row_spec = P(('dp', 'sp'), None, None)

    def local_fn(pair_loc, w_qkvg_s, w_bias_s, w_out_s, w_qkvg_e, w_bias_e, w_out_e, w_one, w_two):
        num_rows, seq_len, channels = pair_loc.shape
        num_heads = w_bias_s.shape[0]
        blk_rows = block_size(num_rows, num_heads * seq_len * seq_len)
        normed = layer_norm(pair_loc)
        bias_loc = jnp.einsum('hc,jkc->hjk', w_bias_s, normed, preferred_element_type=jnp.float32).astype(jnp.bfloat16)
        bias_s = lax.all_gather(bias_loc, 'sp', axis=1, tiled=True)

        def start_block(block_idx):
            normed_blk = lax.dynamic_slice_in_dim(normed, block_idx * blk_rows, blk_rows, axis=0)
            queries, key_vecs, val_vecs, gate_vals = project(normed_blk, w_qkvg_s, num_heads)
            return attend(queries, key_vecs, val_vecs, gate_vals, bias_s, w_out_s, 'rjhd,rkhd->rhjk', 'rhjk,rkhd->rjhd')

        start_upd = lax.map(start_block, jnp.arange(num_rows // blk_rows))
        pair_one = pair_loc + start_upd.reshape(num_rows, seq_len, channels)
        col_major = lax.all_to_all(pair_one.astype(jnp.bfloat16), 'sp', 1, 0, tiled=True)
        normed_c = layer_norm(col_major)
        bias_loc_e = jnp.einsum('hc,kic->hik', w_bias_e, normed_c, preferred_element_type=jnp.float32).astype(jnp.bfloat16)
        bias_e = lax.all_gather(bias_loc_e, 'sp', axis=1, tiled=True)

        def end_block(block_idx):
            normed_blk = lax.dynamic_slice_in_dim(normed_c, block_idx * blk_rows, blk_rows, axis=1)
            pair_blk = lax.dynamic_slice_in_dim(col_major, block_idx * blk_rows, blk_rows, axis=1)
            queries, key_vecs, val_vecs, gate_vals = project(normed_blk, w_qkvg_e, num_heads)
            end_upd = attend(queries, key_vecs, val_vecs, gate_vals, bias_e, w_out_e, 'ijhd,kjhd->jhik', 'jhik,kjhd->ijhd')
            pair_two = pair_blk.astype(jnp.float32) + end_upd
            return (end_upd + transition(pair_two, w_one, w_two)).astype(jnp.bfloat16)

        delta_blocks = lax.map(end_block, jnp.arange(num_rows // blk_rows))
        delta_cols = jnp.moveaxis(delta_blocks, 0, 1).reshape(seq_len, num_rows, channels)
        delta_rows = lax.all_to_all(delta_cols, 'sp', 0, 1, tiled=True)
        return pair_one + delta_rows.astype(jnp.float32)

    return jax.shard_map(local_fn, mesh=mesh, in_specs=(row_spec, P(), P(), P(), P(), P(), P(), P(), P()), out_specs=row_spec, check_vma=False)
```

profile of v0, /device:TPU:1, one launch (start us, length us, event | category | flops | bytes accessed | tf_op | source)
XLA Modules:
  0.0 517.4 jit_solution(16370186673065122340)
XLA Ops:
  6.5 2.5 reduce_sum.72
  9.1 1.4 multiply_reduce_fusion.1
  10.5 1.5 multiply_convert_fusion.4
  12.0 1.0 fusion.65
  13.1 1.7 copy.87
  14.8 69.1 %all-gather.3.cloned.1.call-done = bf16[4,768,768]{2,0,1:T(4,128)(2,1)} async-done(((bf16[4,6,768]{2,0,1:T(4,128)(2,1)}), bf16[4,768,768]{2,0,1:T(4,128)(2,1)}) %all-gather.3.cloned.1.call-update) | async-done | bytes 4718608 | tf_op jit(solution)/shard_map/all_gather | solution.py:58
  83.9 8.4 %copy.88 = bf16[4,768,768]{1,2,0:T(8,128)(2,1)} copy(bf16[4,768,768]{2,0,1:T(4,128)(2,1)} %all-gather.3.cloned.1.call-done) | data formatting | bytes 9437184 | tf_op jit(solution)/shard_map/while | solution.py:65
  92.3 125.3 %while.20 = (s32[]{:T(128)}, f32[2,3,768,128]{3,2,1,0:T(8,128)}, s32[2]{0:T(128)S(1)}, bf16[6,768,128]{2,1,0:T(8,128)(2,1)S(1)}, bf16[128,512]{0,1:T(8,128)(2,1)...) while((s32[]{:T(128)}, f32[2,3,768,128]{3,2,1,0:T(8,128)}, ...), condition=%wide.region_5.6_spmd, body=%wide.region_2.5_spmd.sunk | while | flops 1819322880 | bytes 133538072 | solution.py:65
  94.1 1.8 fusion.134
  96.0 1.3 fusion.135
  97.3 0.9 fusion.136
  98.3 4.5 convert_element_type.176
  102.7 11.8 %fusion.137 = f32[3,4,768]{2,1,0:T(4,128)} fusion(f32[4,768,768]{1,2,0:T(8,128)} %convert_element_type.176, bf16[3,768,4,32]{1,3,2,0:T(8,128)(2,1)S(1)} %bitcast.183, bf16[3,768,4,32]{1,3,2,0:T(8,128)(2,1)S(1)} %bitcast.181), kind=kOutput, calls=%fused_computation.94.clone.1 | convolution fusion | flops 481297152 | bytes 10653696 | tf_op jit(solution)/shard_map/while/body/eval_jaxpr/sub | solution.py:33
  114.6 11.4 %fusion.138 = f32[3,4,768,768]{2,3,1,0:T(8,128)} fusion(bf16[3,768,4,32]{1,3,2,0:T(8,128)(2,1)S(1)} %bitcast.184, bf16[3,768,4,32]{1,3,2,0:T(8,128)(2,1)S(1)} %bitcast.182), kind=kOutput, calls=%fused_computation.98.clone.1 | convolution fusion | flops 452984832 | bytes 29491200 | tf_op jit(solution)/shard_map/while/body/eval_jaxpr/rjhd,rkhd->rhjk/dot_general | solution.py:31
  126.0 26.8 %fusion.139 = bf16[3,768,4,32]{1,3,2,0:T(8,128)(2,1)} fusion(f32[3,768,4,32]{1,3,2,0:T(8,128)} %bitcast.189, bf16[3,768,4,32]{1,3,2,0:T(8,128)(2,1)} %bitcast.194, f32[3,4,768]{2,1,0:T(4,128)} %fusion.137, f32[3,4,768,768]{2,3,1,0:T(8,128)} %fusion.138, f32[4,768,768]{1,2,0:T(8,128)} %convert_element_type.176), kind=kOutput, calls=%fused_computation.13.clone.1 | convolution fusion | flops 503129856 | bytes 40144896 | tf_op jit(solution)/shard_map/while/body/eval_jaxpr/rhjk,rkhd->rjhd/dot_general | solution.py:34
  152.8 2.4 fusion.140
  155.2 0.7 dynamic_slice.31
  156.6 1.8 fusion.134
  158.4 1.3 fusion.135
  159.7 0.9 fusion.136
  160.7 4.5 convert_element_type.176
  165.2 11.8 %fusion.137 = f32[3,4,768]{2,1,0:T(4,128)} fusion(f32[4,768,768]{1,2,0:T(8,128)} %convert_element_type.176, bf16[3,768,4,32]{1,3,2,0:T(8,128)(2,1)S(1)} %bitcast.183, bf16[3,768,4,32]{1,3,2,0:T(8,128)(2,1)S(1)} %bitcast.181), kind=kOutput, calls=%fused_computation.94.clone.1 | convolution fusion | flops 481297152 | bytes 10653696 | tf_op jit(solution)/shard_map/while/body/eval_jaxpr/sub | solution.py:33
  177.0 11.4 %fusion.138 = f32[3,4,768,768]{2,3,1,0:T(8,128)} fusion(bf16[3,768,4,32]{1,3,2,0:T(8,128)(2,1)S(1)} %bitcast.184, bf16[3,768,4,32]{1,3,2,0:T(8,128)(2,1)S(1)} %bitcast.182), kind=kOutput, calls=%fused_computation.98.clone.1 | convolution fusion | flops 452984832 | bytes 29491200 | tf_op jit(solution)/shard_map/while/body/eval_jaxpr/rjhd,rkhd->rhjk/dot_general | solution.py:31
  188.4 26.8 %fusion.139 = bf16[3,768,4,32]{1,3,2,0:T(8,128)(2,1)} fusion(f32[3,768,4,32]{1,3,2,0:T(8,128)} %bitcast.189, bf16[3,768,4,32]{1,3,2,0:T(8,128)(2,1)} %bitcast.194, f32[3,4,768]{2,1,0:T(4,128)} %fusion.137, f32[3,4,768,768]{2,3,1,0:T(8,128)} %fusion.138, f32[4,768,768]{1,2,0:T(8,128)} %convert_element_type.176), kind=kOutput, calls=%fused_computation.13.clone.1 | convolution fusion | flops 503129856 | bytes 40144896 | tf_op jit(solution)/shard_map/while/body/eval_jaxpr/rhjk,rkhd->rjhd/dot_general | solution.py:34
  215.2 2.4 fusion.140
  217.6 2.1 fusion.68
  219.7 0.8 copy.89
  220.6 30.4 %all_to_all.27 = bf16[6,768,128]{2,0,1:T(8,128)(2,1)S(1)} all-to-all(bf16[6,768,128]{2,0,1:T(8,128)(2,1)S(1)} %copy.89), channel_id=1, replica_groups=mesh['dp'=1,'sp'=128] {'sp'}, dimensions={1} | all-to-all | bytes 2359296 | tf_op jit(solution)/shard_map/all_to_all | solution.py:67
  251.0 0.9 convert_reduce_fusion
  252.4 1.8 fusion.64
  255.4 1.3 all_to_all.23
  256.7 3.9 multiply_convert_fusion.3
  260.6 2.3 fusion.66
  263.1 0.8 copy.97
  263.8 62.4 %all-gather.5.cloned.1.call-done = bf16[4,768,768]{2,0,1:T(4,128)(2,1)} async-done(((bf16[4,6,768]{2,0,1:T(4,128)(2,1)}), bf16[4,768,768]{2,0,1:T(4,128)(2,1)}) %all-gather.5.cloned.1.call-update) | async-done | bytes 4718608 | tf_op jit(solution)/shard_map/all_gather | solution.py:70
  326.2 8.4 %copy.98 = bf16[4,768,768]{1,2,0:T(8,128)(2,1)} copy(bf16[4,768,768]{2,0,1:T(4,128)(2,1)} %all-gather.5.cloned.1.call-done) | data formatting | bytes 9437184 | tf_op jit(solution)/shard_map/while | solution.py:80
  334.7 127.4 %while.21 = (s32[]{:T(128)}, bf16[2,768,3,128]{1,3,2,0:T(8,128)(2,1)}, s32[2]{0:T(128)S(1)}, bf16[768,6,128]{2,0,1:T(8,128)(2,1)}, bf16[128,512]{0,1:T(8,128)(2,...) while((s32[]{:T(128)}, ...), condition=%wide.region_13.14_spmd, body=%wide.region_8.13_spmd.sunk | while | flops 2430087936 | bytes 143189376 | solution.py:80
  335.9 1.1 constant_dynamic-slice_fusion.2
  337.3 2.0 fusion.149
  339.7 1.0 fusion.151
  340.6 4.5 convert_element_type.185
  345.1 11.2 %fusion.152 = f32[3,4,768]{2,1,0:T(4,128)S(1)} fusion(f32[4,768,768]{1,2,0:T(8,128)} %convert_element_type.185, bf16[768,3,4,32]{0,3,2,1:T(8,128)(2,1)S(1)} %bitcast.187, bf16[768,3,4,32]{0,3,2,1:T(8,128)(2,1)S(1)} %bitcast.185), kind=kOutput, calls=%fused_computation.97.clone.1 | convolution fusion | flops 481297152 | bytes 10653696 | tf_op jit(solution)/shard_map/while/body/eval_jaxpr/sub | solution.py:33
  356.3 11.4 %fusion.153 = f32[3,4,768,768]{2,3,1,0:T(8,128)} fusion(bf16[768,3,4,32]{0,3,2,1:T(8,128)(2,1)S(1)} %bitcast.188, bf16[768,3,4,32]{0,3,2,1:T(8,128)(2,1)S(1)} %bitcast.186), kind=kOutput, calls=%fused_computation.99.clone.1 | convolution fusion | flops 452984832 | bytes 29491200 | tf_op jit(solution)/shard_map/while/body/eval_jaxpr/ijhd,kjhd->jhik/dot_general | solution.py:31
  367.8 26.3 %fusion.154 = bf16[768,3,4,32]{0,3,2,1:T(8,128)(2,1)} fusion(f32[768,3,4,32]{0,3,2,1:T(8,128)S(1)} %bitcast.190, bf16[768,3,4,32]{0,3,2,1:T(8,128)(2,1)} %bitcast.195, f32[3,4,768]{2,1,0:T(4,128)S(1)} %fusion.152, f32[3,4,768,768]{2,3,1,0:T(8,128)} %fusion.153, f32[4,768,768]{1,2,0:T(8,128)} %convert_element_type.185), kind=kOutput, calls=%fused_computation.43.clone.1 | convolution fusion | flops 503129856 | bytes 40144896 | tf_op jit(solution)/shard_map/while/body/eval_jaxpr/jhik,kjhd->ijhd/dot_general | solution.py:34
  394.1 1.5 fusion.155
  395.9 1.4 fusion.156
  397.4 1.0 copy-done.8
  399.6 1.1 constant_dynamic-slice_fusion.2
  401.0 2.0 fusion.149
  403.4 1.0 fusion.151
  404.3 4.5 convert_element_type.185
  408.8 11.2 %fusion.152 = f32[3,4,768]{2,1,0:T(4,128)S(1)} fusion(f32[4,768,768]{1,2,0:T(8,128)} %convert_element_type.185, bf16[768,3,4,32]{0,3,2,1:T(8,128)(2,1)S(1)} %bitcast.187, bf16[768,3,4,32]{0,3,2,1:T(8,128)(2,1)S(1)} %bitcast.185), kind=kOutput, calls=%fused_computation.97.clone.1 | convolution fusion | flops 481297152 | bytes 10653696 | tf_op jit(solution)/shard_map/while/body/eval_jaxpr/sub | solution.py:33
  420.0 11.4 %fusion.153 = f32[3,4,768,768]{2,3,1,0:T(8,128)} fusion(bf16[768,3,4,32]{0,3,2,1:T(8,128)(2,1)S(1)} %bitcast.188, bf16[768,3,4,32]{0,3,2,1:T(8,128)(2,1)S(1)} %bitcast.186), kind=kOutput, calls=%fused_computation.99.clone.1 | convolution fusion | flops 452984832 | bytes 29491200 | tf_op jit(solution)/shard_map/while/body/eval_jaxpr/ijhd,kjhd->jhik/dot_general | solution.py:31
  431.4 26.3 %fusion.154 = bf16[768,3,4,32]{0,3,2,1:T(8,128)(2,1)} fusion(f32[768,3,4,32]{0,3,2,1:T(8,128)S(1)} %bitcast.190, bf16[768,3,4,32]{0,3,2,1:T(8,128)(2,1)} %bitcast.195, f32[3,4,768]{2,1,0:T(4,128)S(1)} %fusion.152, f32[3,4,768,768]{2,3,1,0:T(8,128)} %fusion.153, f32[4,768,768]{1,2,0:T(8,128)} %convert_element_type.185), kind=kOutput, calls=%fused_computation.43.clone.1 | convolution fusion | flops 503129856 | bytes 40144896 | tf_op jit(solution)/shard_map/while/body/eval_jaxpr/jhik,kjhd->ijhd/dot_general | solution.py:34
  457.8 1.5 fusion.155
  459.6 1.4 fusion.156
  461.1 1.0 copy-done.8
  462.1 2.1 copy.102
  464.1 30.8 %all_to_all.28 = bf16[768,6,128]{2,1,0:T(8,128)(2,1)S(1)} all-to-all(bf16[768,6,128]{2,1,0:T(8,128)(2,1)S(1)} %copy.102), channel_id=1, replica_groups=mesh['dp'=1,'sp'=128] {'sp'}, dimensions={0} | all-to-all | bytes 2359296 | tf_op jit(solution)/shard_map/all_to_all | solution.py:82
  495.0 1.6 copy_convert_fusion
  496.5 2.5 reshape.110
  499.0 3.1 copy.104
  502.1 4.1 reshape.109
  506.3 4.4 fusion.67
  (92 shorter events, 5.5 us)
Async XLA Ops:
  6.5 5.5 %copy-start = (bf16[4,128]{1,0:T(4,128)(2,1)S(1)}, bf16[4,128]{1,0:T(4,128)(2,1)}, u32[]{:S(2)}) copy-start(bf16[4,128]{1,0:T(4,128)(2,1)} %param.15) | copy-start | bytes 3076
  6.5 2.5 copy-start.2
  6.5 77.3 %all-gather.3.cloned.1.call-start = ((), (), s32[]{:S(2)}) async-start(), calls=%async_computation.2 | async-start | bytes 4755456 | tf_op jit(solution)/shard_map/all_gather | solution.py:58
  13.1 313.1 %all-gather.5.cloned.1.call-start = ((), (), s32[]{:S(2)}) async-start(), calls=%async_computation.3 | async-start | bytes 4755456 | tf_op jit(solution)/shard_map/all_gather | solution.py:70
  92.3 125.3 %copy-start.3 = (f32[6,768,128]{2,1,0:T(8,128)S(1)}, f32[6,768,128]{2,1,0:T(8,128)}, u32[]{:S(2)}) copy-start(f32[6,768,128]{2,1,0:T(8,128)} %param.13) | copy-start | bytes 7077892
  92.3 3.6 copy-start.5
  94.1 4.1 slice-start.2
  94.1 4.1 slice-start.3
  126.0 29.2 %copy-start.6 = (bf16[6,768,128]{2,1,0:T(8,128)(2,1)S(1)}, bf16[6,768,128]{2,1,0:T(8,128)(2,1)}, u32[]{:S(2)}) copy-start(bf16[6,768,128]{2,1,0:T(8,128)(2,1)} %copy-done.5) | copy-start | bytes 3538948 | tf_op jit(solution)/shard_map/while
  155.2 3.2 copy-start.5
  156.5 4.2 slice-start.2
  156.5 4.2 slice-start.3
  188.4 29.2 %copy-start.6 = (bf16[6,768,128]{2,1,0:T(8,128)(2,1)S(1)}, bf16[6,768,128]{2,1,0:T(8,128)(2,1)}, u32[]{:S(2)}) copy-start(bf16[6,768,128]{2,1,0:T(8,128)(2,1)} %copy-done.5) | copy-start | bytes 3538948 | tf_op jit(solution)/shard_map/while
  255.4 5.2 copy-start.11
  256.7 6.2 %copy-start.10 = (bf16[128,128]{1,0:T(8,128)(2,1)S(1)}, bf16[128,128]{1,0:T(8,128)(2,1)}, u32[]{:S(2)}) copy-start(bf16[128,128]{1,0:T(8,128)(2,1)} %param.19) | copy-start | bytes 98308
  256.7 6.3 %copy-start.9 = (bf16[128,512]{1,0:T(8,128)(2,1)S(1)}, bf16[128,512]{1,0:T(8,128)(2,1)}, u32[]{:S(2)}) copy-start(bf16[128,512]{1,0:T(8,128)(2,1)} %param.17) | copy-start | bytes 393220
  337.1 3.6 slice-start
  337.3 3.3 slice-start.1
  394.1 1.8 copy-start.7
  394.1 1.8 copy-start.12
  394.1 1.8 copy-start.13
  397.3 1.0 copy-start.8
  400.8 3.6 slice-start
  401.0 3.3 slice-start.1
  457.8 1.8 copy-start.7
  457.8 1.8 copy-start.12
  457.8 1.8 copy-start.13
  461.0 1.0 copy-start.8
  502.1 4.1 copy-start.4
  502.1 8.5 %copy-start.1 = (bf16[4,128]{1,0:T(4,128)(2,1)S(1)}, bf16[4,128]{1,0:T(4,128)(2,1)}, u32[]{:S(2)}) copy-start(bf16[4,128]{1,0:T(4,128)(2,1)} %param.15) | copy-start | bytes 3076
Sparse Core Ops, SparseCore 0:
  13.2 70.6 all-gather.2
  263.0 63.1 all-gather.4
where the time goes:
time: 518 us; the launch traced here: 517 us
  matrix products  220 us (42%)
  waiting for transfers between devices  132 us (25%)
  blocking collectives  61.3 us (12%)
  local copies, waits for them, and re-layouts  46.1 us (9%)
  other arithmetic  41.7 us (8%)
  between operations  13.6 us (3%)
    dot_general x4, matrix products, attend(): jnp.einsum(mix_form, attn_prob, val_vecs, preferred_element_type=jnp.floa...  106 us
    all_gather x1, waiting for transfers between devices, local_fn(): bias_s = lax.all_gather(bias_loc, 'sp', axis=1, tiled=True)  69.1 us
    all_gather x1, waiting for transfers between devices, local_fn(): bias_e = lax.all_gather(bias_loc_e, 'sp', axis=1, tiled=True)  62.4 us
    sub x4, matrix products, attend(): attn_prob = jax.nn.softmax(scores, axis=-1).astype(jnp.bfloat16)  46.1 us
    dot_general x4, matrix products, attend(): jnp.einsum(score_form, queries, key_vecs, preferred_element_type=jnp.floa...  45.6 us
    all_to_all x1, blocking collectives, local_fn(): delta_rows = lax.all_to_all(delta_cols, 'sp', 0, 1, tiled=True)  30.8 us
    all_to_all x1, blocking collectives, local_fn(): lax.all_to_all(pair_one.astype(jnp.bfloat16), 'sp', 1, 0, tiled=True)  30.4 us
    convert_element_type x4, other arithmetic, attend(): scores = scores * head_dim ** (-0.5) + bias_full.astype(jnp.float32)  17.9 us
  transfers between devices with their start and end apart: 2, of which 2 were waited for; matrix products, arithmetic and copies ran while one was open for 0% of the time, Pallas kernels for 0%

commit v1 on v0

v1 whole, which is shorter than its diff:
```python
import functools
import math
import jax
import jax.numpy as jnp
from jax import lax
from jax.experimental import pallas as pl
from jax.experimental.pallas import tpu as pltpu
from jax.sharding import PartitionSpec as P

F32, BF16 = jnp.float32, jnp.bfloat16
LOG2E = math.log2(math.e)
EPS = 1e-5

def ln(x):
    mu = jnp.mean(x, axis=-1, keepdims=True)
    c = x - mu
    var = jnp.mean(c * c, axis=-1, keepdims=True)
    return (c * lax.rsqrt(var + EPS)).astype(BF16)

def dotf(a, b):
    return jnp.dot(a, b, preferred_element_type=F32)

def dot_nt(a, b):
    return lax.dot_general(a, b, (((1,), (1,)), ((), ())), preferred_element_type=F32)

def attn_kernel(end, n, heads, nq, x_ref, bias_ref, wqvg_ref, wkT_ref, wo_ref, w1_ref, w2_ref, o_ref, bf_ref, q_ref, g_ref, kT_ref, v_ref, s_ref):
    c = x_ref.shape[-1]
    hd = c // heads
    @pl.when(pl.program_id(0) == 0)
    def _():
        for h in range(heads):
            def cvt(r, _):
                rows = pl.ds(pl.multiple_of(r * 64, 64), 64)
                bf_ref[h, rows, :] = bias_ref[h, rows, :].astype(F32) * LOG2E
                return 0
            lax.fori_loop(0, n // 64, cvt, 0)
        v_ref[:, c:] = jnp.ones((n, c), BF16)
    x = x_ref[0].astype(F32)
    u = ln(x)
    kT_ref[...] = dot_nt(wkT_ref[...], u).astype(BF16)
    pr = dotf(u, wqvg_ref[...])
    q_ref[...] = pr[:, :c].astype(BF16)
    v_ref[:, :c] = pr[:, c:2 * c].astype(BF16)
    g_ref[...] = jax.nn.sigmoid(pr[:, 2 * c:])
    scale = hd ** -0.5 * LOG2E
    def block(b, _):
        rows = pl.ds(pl.multiple_of(b * nq, nq), nq)
        qb = q_ref[rows, :]
        lane = lax.broadcasted_iota(jnp.int32, (nq, c), 1) // hd
        res = jnp.zeros((nq, c), F32)
        for h in range(heads):
            qm = jnp.where(lane == h, qb, jnp.zeros_like(qb))
            s = dotf(qm, kT_ref[...])
            t = s * scale + bf_ref[h, rows, :]
            m = jnp.max(t, axis=-1, keepdims=True)
            p = jnp.exp2(t - m).astype(BF16)
            o = dotf(p, v_ref[...])
            res = jnp.where(lane == h, o[:, :c] / o[:, c:], res)
        og = (res * g_ref[rows, :]).astype(BF16)
        upd = dotf(og, wo_ref[...])
        if not end:
            o_ref[0, rows, :] = x_ref[0, rows, :] + upd
        else:
            two = x_ref[0, rows, :].astype(F32) + upd
            hid = jnp.maximum(dotf(ln(two), w1_ref[...]), 0).astype(BF16)
            o_ref[0, rows, :] = (upd + dotf(hid, w2_ref[...])).astype(BF16)
        return 0
    lax.fori_loop(0, n // nq, block, 0)

def attention(x, bias, wqkvg, wo, w1, w2, end, nq=384):
    rows, n, c = x.shape
    heads = bias.shape[0]
    wqvg = jnp.concatenate([wqkvg[:, :c], wqkvg[:, 2 * c:]], axis=1)
    wkT = wqkvg[:, c:2 * c].T
    full = lambda a: pl.BlockSpec(a.shape, lambda i: (0,) * a.ndim, pipeline_mode=pl.Buffered(1))
    return pl.pallas_call(
        functools.partial(attn_kernel, end, n, heads, nq),
        grid=(rows,),
        in_specs=[pl.BlockSpec((1, n, c), lambda i: (i, 0, 0)), full(bias), full(wqvg), full(wkT), full(wo), full(w1), full(w2)],
        out_specs=pl.BlockSpec((1, n, c), lambda i: (i, 0, 0)),
        out_shape=jax.ShapeDtypeStruct((rows, n, c), BF16 if end else F32),
        scratch_shapes=[pltpu.VMEM((heads, n, n), F32), pltpu.VMEM((n, c), BF16), pltpu.VMEM((n, c), F32), pltpu.VMEM((c, n), BF16), pltpu.VMEM((n, 2 * c), BF16), pltpu.VMEM((8, 128), F32)],
        compiler_params=pltpu.CompilerParams(vmem_limit_bytes=60 * 2**20),
    )(x, bias, wqvg, wkT, wo, w1, w2)


def solution(mesh):
    row_spec = P(('dp', 'sp'), None, None)

    def local_fn(z, wqkvg_s, wb_s, wo_s, wqkvg_e, wb_e, wo_e, w1, w2):
        bias_s = jnp.einsum('hc,jkc->hjk', wb_s, ln(z), preferred_element_type=F32).astype(BF16)
        bias_s = lax.all_gather(bias_s, 'sp', axis=1, tiled=True)
        z1 = attention(z, bias_s, wqkvg_s, wo_s, w1, w2, False)
        cols = lax.all_to_all(z1.astype(BF16), 'sp', 1, 0, tiled=True)
        cols = jnp.swapaxes(cols, 0, 1)
        bias_e = jnp.einsum('hc,ikc->hik', wb_e, ln(cols.astype(F32)), preferred_element_type=F32).astype(BF16)
        bias_e = lax.all_gather(bias_e, 'sp', axis=1, tiled=True)
        delta = attention(cols, bias_e, wqkvg_e, wo_e, w1, w2, True)
        delta = lax.all_to_all(jnp.swapaxes(delta, 0, 1), 'sp', 0, 1, tiled=True)
        return z1 + delta.astype(F32)

    return jax.shard_map(local_fn, mesh=mesh, in_specs=(row_spec,) + (P(),) * 8, out_specs=row_spec, check_vma=False)
```

time: 518 us -> 326 us (0.63)
  matrix products: 220 us -> 5.38 us
  Pallas kernels: 0 us -> 75 us
  other arithmetic: 41.7 us -> 13.9 us
  local copies, waits for them, and re-layouts: 46.1 us -> 25 us
    dot_general x20 -> x2, matrix products: 174 us -> 5.38 us  [the longest x1 2.7 us: local_fn(): jnp.einsum('hc,jkc->hjk', wb_s, ln(z), preferred_element_type=F32)]
    pallas_call x0 -> x2, Pallas kernels: none -> 75 us  [attention(): pl.pallas_call(functools.partial(attn_kernel, end, n, heads, nq), grid=(r...]
    sub x4 -> x0, matrix products: 46.1 us -> none  [attend(): attn_prob = jax.nn.softmax(scores, axis=-1).astype(jnp.bfloat16)]
    convert_element_type x8 -> x2, other arithmetic: 26.9 us -> 3.38 us  [the longest x1 1.82 us: local_fn(): cols = lax.all_to_all(z1.astype(BF16), 'sp', 1, 0, tiled=True)]
    while x45 -> x0, local copies, waits for them, and re-layouts: 21.5 us -> none  [the longest x2 10.1 us: local_fn(): start_upd = lax.map(start_block, jnp.arange(num_rows // blk_rows))]
    all_gather x0 -> x2, local copies, waits for them, and re-layouts: none -> 10.2 us  [the longest x1 5.1 us: local_fn(): bias_s = lax.all_gather(bias_s, 'sp', axis=1, tiled=True)]
    dynamic_slice x8 -> x0, local copies, waits for them, and re-layouts: 5.29 us -> none  [the longest x4 2.72 us: end_block(): lax.dynamic_slice_in_dim(col_major, block_idx * blk_rows, blk_rows, axis=1)]
  transfers between devices with their start and end apart: 2 -> 2, of which waited for: 2 -> 2; matrix products, arithmetic and copies ran while one was open for 0% -> 1% of each run, Pallas kernels for 0% -> 0%
where the time goes in v1:
time: 326 us; the launch traced here: 325 us
  waiting for transfers between devices  131 us (40%)
  Pallas kernels  75 us (23%)
  blocking collectives  61.3 us (19%)
  local copies, waits for them, and re-layouts  25 us (8%)
  other arithmetic  13.9 us (4%)
  between operations  13.6 us (4%)
  matrix products  5.38 us (2%)
    pallas_call x2, Pallas kernels, attention(): pl.pallas_call(functools.partial(attn_kernel, end, n, heads, nq), grid=(r...  75 us
    all_gather x1, waiting for transfers between devices, local_fn(): bias_s = lax.all_gather(bias_s, 'sp', axis=1, tiled=True)  69.4 us
    all_gather x1, waiting for transfers between devices, local_fn(): bias_e = lax.all_gather(bias_e, 'sp', axis=1, tiled=True)  61.9 us
    all_to_all x1, blocking collectives, local_fn(): delta = lax.all_to_all(jnp.swapaxes(delta, 0, 1), 'sp', 0, 1, tiled=True)  30.8 us
    all_to_all x1, blocking collectives, local_fn(): cols = lax.all_to_all(z1.astype(BF16), 'sp', 1, 0, tiled=True)  30.4 us
    convert_element_type x3, local copies, waits for them, and re-layouts, local_fn(): return z1 + delta.astype(F32)  9.67 us
  transfers between devices with their start and end apart: 2, of which 2 were waited for; matrix products, arithmetic and copies ran while one was open for 1% of the time, Pallas kernels for 0%

profile of v1, /device:TPU:1, one launch (start us, length us, event | category | flops | bytes accessed | tf_op | source)
XLA Modules:
  0.0 325.4 jit_solution(6331331580013496155)
XLA Ops:
  6.5 0.0 copy-start
  6.5 0.0 copy-start.1
  6.5 0.0 all-gather.3.cloned.1.call-start
  6.5 2.5 reduce_sum.36
  9.1 0.0 copy-done.1
  9.1 0.0 copy-start.4
  9.1 0.0 slice-start
  9.1 1.4 multiply_reduce_fusion
  10.6 0.0 copy-done
  10.6 2.7 fusion.15
  13.3 0.0 all-gather.3.cloned.1.call-update
  13.3 0.0 all-gather.5.cloned.1.call-start
  13.3 0.0 copy-done.4
  13.4 0.7 copy.44
  14.1 0.0 slice-done
  14.1 0.6 pad_maximum_fusion.wqvg_ref
  14.7 69.4 %all-gather.3.cloned.1.call-done = bf16[4,768,768]{2,0,1:T(4,128)(2,1)} async-done(((bf16[4,6,768]{2,0,1:T(4,128)(2,1)}), bf16[4,768,768]{2,0,1:T(4,128)(2,1)}) %all-gather.3.cloned.1.call-update) | async-done | bytes 4718608 | tf_op jit(solution)/shard_map/all_gather | solution.py:92
  84.1 5.1 %copy.33.bias_ref = bf16[4,768,768]{2,1,0:T(8,128)(2,1)} copy(bf16[4,768,768]{2,0,1:T(4,128)(2,1)} %all-gather.3.cloned.1.call-done) | data formatting | bytes 9437184 | tf_op jit(solution)/shard_map/all_gather | solution.py:92
  89.2 33.9 %shard_map.91 = f32[6,768,128]{2,1,0:T(8,128)} custom-call(f32[6,768,128]{2,1,0:T(8,128)} %x_ref.1, bf16[4,768,768]{2,1,0:T(8,128)(2,1)} %copy.33.bias_ref, bf16[128,384]{1,0:T(8,128)(2,1)} %pad_maximum_fusion.wqvg_ref, bf16[128,128]{1,0:T(8,128)(2,1)} %bitcast.34, bf16[128,128]{1,0:T(8,128)(2,1)} %wo_ref.2, bf16[128,512]{1,0:T(8,128)(2,1)} %w1_ref.3, ...), custom_call_target="tpu_custom_call" | custom-call | tf_op jit(solution)/shard_map/pallas_call | solution.py:76
  123.1 1.8 convert_element_type.39
  124.9 0.8 copy.34
  125.7 30.4 %all_to_all.27 = bf16[6,768,128]{2,0,1:T(8,128)(2,1)S(1)} all-to-all(bf16[6,768,128]{2,0,1:T(8,128)(2,1)S(1)} %copy.34), channel_id=1, replica_groups=mesh['dp'=1,'sp'=128] {'sp'}, dimensions={1} | all-to-all | bytes 2359296 | tf_op jit(solution)/shard_map/all_to_all | solution.py:94
  156.2 0.3 copy.36
  156.5 0.0 copy-start.6
  156.5 0.5 all_to_all.23
  156.9 0.0 copy-start.3
  156.9 0.0 copy-start.5
  157.0 0.0 slice-start.1
  157.0 0.4 convert_reduce_fusion
  157.4 1.4 fusion.2
  158.8 0.0 copy-done.6
  158.8 2.7 fusion.16
  161.5 0.0 all-gather.5.cloned.1.call-update
  161.5 0.0 copy-done.3
  161.6 0.0 copy-done.5
  161.6 0.7 copy.45
  162.3 0.0 slice-done.1
  162.3 0.6 pad_maximum_fusion.1.wqvg_ref
  162.9 61.9 %all-gather.5.cloned.1.call-done = bf16[4,768,768]{2,0,1:T(4,128)(2,1)} async-done(((bf16[4,6,768]{2,0,1:T(4,128)(2,1)}), bf16[4,768,768]{2,0,1:T(4,128)(2,1)}) %all-gather.5.cloned.1.call-update) | async-done | bytes 4718608 | tf_op jit(solution)/shard_map/all_gather | solution.py:97
  224.8 5.1 %copy.38.bias_ref = bf16[4,768,768]{2,1,0:T(8,128)(2,1)} copy(bf16[4,768,768]{2,0,1:T(4,128)(2,1)} %all-gather.5.cloned.1.call-done) | data formatting | bytes 9437184 | tf_op jit(solution)/shard_map/all_gather | solution.py:97
  229.9 41.1 %shard_map.92 = bf16[6,768,128]{2,1,0:T(8,128)(2,1)} custom-call(bf16[6,768,128]{2,1,0:T(8,128)(2,1)} %bitcast.29, bf16[4,768,768]{2,1,0:T(8,128)(2,1)} %copy.38.bias_ref, bf16[128,384]{1,0:T(8,128)(2,1)} %pad_maximum_fusion.1.wqvg_ref, bf16[128,128]{1,0:T(8,128)(2,1)} %bitcast.33, bf16[128,128]{1,0:T(8,128)(2,1)} %wo_ref.3, bf16[128,512]{1,0:T(8,128)(2,1)} %w1_ref.3, ...), custom_call_target="tpu_custom_call" | custom-call | tf_op jit(solution)/shard_map/pallas_call | solution.py:76
  271.0 2.1 copy.39
  273.1 30.8 %all_to_all.28 = bf16[768,6,128]{2,1,0:T(8,128)(2,1)S(1)} all-to-all(bf16[768,6,128]{2,1,0:T(8,128)(2,1)S(1)} %copy.39), channel_id=1, replica_groups=mesh['dp'=1,'sp'=128] {'sp'}, dimensions={0} | all-to-all | bytes 2359296 | tf_op jit(solution)/shard_map/all_to_all | solution.py:99
  303.9 1.6 copy_convert_fusion
  305.4 2.5 reshape.29
  307.9 3.1 copy.41
  311.0 0.0 copy-start.2
  311.0 4.1 %reshape.28 = f32[6,768,128]{2,1,0:T(8,128)} reshape(f32[6,128,6,128]{3,2,1,0:T(8,128)} %copy.41) | data formatting | bytes 4718592 | tf_op jit(solution)/shard_map/convert_element_type | solution.py:100
  315.1 0.0 copy-done.2
  315.1 3.5 %add.21 = f32[6,768,128]{2,1,0:T(8,128)} add(f32[6,768,128]{2,1,0:T(8,128)S(1)} %copy-done.2, f32[6,768,128]{2,1,0:T(8,128)} %reshape.28) | non-fusion elementwise | flops 589824 | bytes 7077888 | tf_op jit(solution)/shard_map/add | solution.py:100
  (6 shorter events, 0.0 us)
Async XLA Ops:
  6.5 4.0 %copy-start = (bf16[4,128]{1,0:T(4,128)(2,1)S(1)}, bf16[4,128]{1,0:T(4,128)(2,1)}, u32[]{:S(2)}) copy-start(bf16[4,128]{1,0:T(4,128)(2,1)} %param.11) | copy-start | bytes 3076
  6.5 2.5 copy-start.1
  6.5 77.5 %all-gather.3.cloned.1.call-start = ((), (), s32[]{:S(2)}) async-start(), calls=%async_computation.2 | async-start | bytes 4755456 | tf_op jit(solution)/shard_map/all_gather | solution.py:92
  9.1 4.3 %copy-start.4 = (bf16[128,512]{1,0:T(8,128)(2,1)S(1)}, bf16[128,512]{1,0:T(8,128)(2,1)}, u32[]{:S(2)}) copy-start(bf16[128,512]{1,0:T(8,128)(2,1)} %param.10) | copy-start | bytes 393220
  9.1 5.0 %slice-start = ((bf16[128,512]{1,0:T(8,128)(2,1)}), bf16[128,256]{1,0:T(8,128)(2,1)S(1)}, s32[]{:S(2)}) async-start(bf16[128,512]{1,0:T(8,128)(2,1)} %param.10), calls=%async_computation.4 | async-start | bytes 131072 | tf_op jit(solution)/shard_map/slice | solution.py:73
  13.3 211.5 %all-gather.5.cloned.1.call-start = ((), (), s32[]{:S(2)}) async-start(), calls=%async_computation.3 | async-start | bytes 4755456 | tf_op jit(solution)/shard_map/all_gather | solution.py:97
  156.5 2.4 copy-start.6
  156.9 4.6 %copy-start.3 = (bf16[768,6,128]{2,0,1:T(8,128)(2,1)}, bf16[768,6,128]{2,0,1:T(8,128)(2,1)S(1)}, u32[]{:S(2)}) copy-start(bf16[768,6,128]{2,0,1:T(8,128)(2,1)S(1)} %all_to_all.23) | copy-start | bytes 3538948
  156.9 4.6 %copy-start.5 = (bf16[128,512]{1,0:T(8,128)(2,1)S(1)}, bf16[128,512]{1,0:T(8,128)(2,1)}, u32[]{:S(2)}) copy-start(bf16[128,512]{1,0:T(8,128)(2,1)} %param.13) | copy-start | bytes 393220
  157.0 5.3 %slice-start.1 = ((bf16[128,512]{1,0:T(8,128)(2,1)}), bf16[128,256]{1,0:T(8,128)(2,1)S(1)}, s32[]{:S(2)}) async-start(bf16[128,512]{1,0:T(8,128)(2,1)} %param.13), calls=%async_computation.5 | async-start | bytes 131072 | tf_op jit(solution)/shard_map/slice | solution.py:73
  311.0 4.1 %copy-start.2 = (f32[6,768,128]{2,1,0:T(8,128)S(1)}, f32[6,768,128]{2,1,0:T(8,128)}, u32[]{:S(2)}) copy-start(f32[6,768,128]{2,1,0:T(8,128)} %shard_map.91) | copy-start | bytes 7077892
Sparse Core Ops, SparseCore 0:
  13.4 70.6 all-gather.2
  161.7 63.1 all-gather.4

commit v2 on v1

v2 whole, which is shorter than its diff:
```python
import functools
import math
import random
import jax
import jax.numpy as jnp
import numpy as np
from jax import lax
from jax.experimental import pallas as pl
from jax.experimental.pallas import tpu as pltpu
from jax.sharding import PartitionSpec as P

F32, BF16 = jnp.float32, jnp.bfloat16
LOG2E = math.log2(math.e)
EPS = 1e-5
MESH = pl.DeviceIdType.MESH
STRIDES = (2, 8, 32)

def rcopy(src, dst, ssem, rsem, peer):
    return pltpu.make_async_remote_copy(src_ref=src, dst_ref=dst, send_sem=ssem, recv_sem=rsem, device_id={'sp': peer}, device_id_type=MESH)

def bytes_wait(ref, sem):
    pltpu.make_async_copy(ref, ref, sem).wait()

def coord(me, s):
    return lax.rem(me // s, 4)

def ring(me, s, t):
    cc = coord(me, s)
    return me + (lax.rem(cc + t, 4) - cc) * s

def gather_start(me, x_ref, o_ref, ssem, rsem):
    for c in range(3):
        sa = STRIDES[c]
        for t in (1, 3, 2):
            rcopy(x_ref.at[c], o_ref.at[c, me], ssem, rsem.at[c, 0], ring(me, sa, t)).start()
        rcopy(x_ref.at[c], o_ref.at[c, me], ssem, rsem.at[c, 5], me ^ 1).start()

def gather_rest(me, x_ref, o_ref, ssem, rsem):
    dims = [(STRIDES[c], STRIDES[(c + 1) % 3], STRIDES[(c + 2) % 3]) for c in range(3)]
    def push(c, d, peer, k):
        rcopy(o_ref.at[c, d], o_ref.at[c, d], ssem, rsem.at[c, k], peer).start()
    partner = me ^ 1
    for c in range(3):
        sa, sb, sd = dims[c]
        bytes_wait(o_ref.at[c, pl.ds(0, 3)], rsem.at[c, 0])
        base = me - coord(me, sa) * sa
        def body(j, _):
            d = base + j * sa
            for t in (1, 3, 2):
                push(c, d, ring(me, sb, t), 1)
            @pl.when(d != me)
            def _():
                push(c, d, partner, 5)
            return 0
        lax.fori_loop(0, 4, body, 0)
    for c in range(3):
        sa, sb, sd = dims[c]
        bytes_wait(o_ref.at[c, pl.ds(0, 12)], rsem.at[c, 1])
        cb = coord(me, sb)
        base = me - coord(me, sa) * sa - cb * sb
        def body(j, _):
            jb = j // 4
            d = base + lax.rem(j, 4) * sa + jb * sb
            push(c, d, ring(me, sd, 1), 2)
            push(c, d, ring(me, sd, 3), 3)
            @pl.when(jb != cb)
            def _():
                push(c, d, partner, 5)
            return 0
        lax.fori_loop(0, 16, body, 0)
    for side in range(2):
        for c in range(3):
            sa, sb, sd = dims[c]
            bytes_wait(o_ref.at[c, pl.ds(0, 16)], rsem.at[c, 2 + side])
            src = ring(me, sd, 3 if side == 0 else 1)
            base = src - coord(me, sa) * sa - coord(me, sb) * sb
            to = ring(me, sd, 1 if side == 0 else 3)
            def body(j, _):
                d = base + lax.rem(j, 4) * sa + (j // 4) * sb
                @pl.when(j // 8 == side)
                def _():
                    push(c, d, to, 4)
                push(c, d, partner, 5)
                return 0
            lax.fori_loop(0, 16, body, 0)
    for c in range(3):
        sa, sb, sd = dims[c]
        bytes_wait(o_ref.at[c, pl.ds(0, 16)], rsem.at[c, 4])
        src = ring(me, sd, 2)
        base = src - coord(me, sa) * sa - coord(me, sb) * sb
        def body(j, _):
            push(c, base + lax.rem(j, 4) * sa + (j // 4) * sb, partner, 5)
            return 0
        lax.fori_loop(0, 16, body, 0)
    for c in range(3):
        bytes_wait(o_ref.at[c, pl.ds(0, 64)], rsem.at[c, 5])
    for c in range(3):
        bytes_wait(o_ref.at[c, pl.ds(0, 127)], ssem)

def exchange_start(me, h_ref, r_ref, n, ssem, rsem):
    for k in send_order(n):
        d = me ^ k
        rcopy(h_ref.at[d], r_ref.at[me], ssem, rsem, d).start()

def exchange_wait(r_ref, n, ssem, rsem):
    bytes_wait(r_ref.at[pl.ds(0, n - 1)], rsem)
    bytes_wait(r_ref.at[pl.ds(0, n - 1)], ssem)

def a2a_kernel(n, h_ref, r_ref, lsem, ssem, rsem):
    me = lax.axis_index('sp')
    own = pltpu.make_async_copy(h_ref.at[me], r_ref.at[me], lsem)
    own.start()
    exchange_start(me, h_ref, r_ref, n, ssem, rsem)
    own.wait()
    exchange_wait(r_ref, n, ssem, rsem)

def all_to_all(h, n):
    anyspec = pl.BlockSpec(memory_space=pl.ANY)
    return pl.pallas_call(functools.partial(a2a_kernel, n), in_specs=[anyspec], out_specs=anyspec,
        out_shape=jax.ShapeDtypeStruct(h.shape, h.dtype),
        scratch_shapes=[pltpu.SemaphoreType.DMA, pltpu.SemaphoreType.DMA, pltpu.SemaphoreType.DMA],
        compiler_params=pltpu.CompilerParams(has_side_effects=True), name='exchange')(h)


def send_order(n):
    groups = {}
    for k in range(1, n):
        x, y, z = (k >> 1) & 3, (k >> 3) & 3, (k >> 5) & 3
        g = (0, x) if x else (1, y) if y else (2, z)
        groups.setdefault(g, []).append(k)
    slots = []
    for ks in groups.values():
        ks = sorted(ks, key=lambda k: random.Random(k).random())
        slots += [((i + 0.5) / len(ks), k) for i, k in enumerate(ks)]
    return [k for _, k in sorted(slots)]


def ln(x):
    mu = jnp.mean(x, axis=-1, keepdims=True)
    c = x - mu
    var = jnp.mean(c * c, axis=-1, keepdims=True)
    return (c * lax.rsqrt(var + EPS)).astype(BF16)


def dotf(a, b):
    return jnp.dot(a, b, preferred_element_type=F32)


def dot_nt(a, b):
    return lax.dot_general(a, b, (((1,), (1,)), ((), ())), preferred_element_type=F32)


def pack_matrix(per, pad, devs):
    m = np.zeros((devs, pad, per, devs, per), np.float32)
    for d in range(devs):
        for a in range(per):
            for b in range(per):
                m[d, a * per + b, a, d, b] = 1
    return jnp.asarray(m.reshape(devs * pad, per * devs * per), BF16)


def unpack_matrix(per, pad, devs):
    m = np.zeros((per, devs, per, devs, pad), np.float32)
    for d in range(devs):
        for a in range(per):
            for b in range(per):
                m[b, d, a, d, a * per + b] = 1
    return jnp.asarray(m.reshape(per * devs * per, devs * pad), BF16)


def bias_matrix(per, heads, devs):
    m = np.zeros((heads, devs, per, devs, per, heads), np.float32)
    for d in range(devs):
        for a in range(per):
            for h in range(heads):
                m[h, d, a, d, a, h] = 1
    return jnp.asarray(m.reshape(heads * devs * per, devs * per * heads), BF16)


def pack_rows(src_ref, pm_ref, out_ref, devs):
    per, n, c = src_ref.shape
    pad = out_ref.shape[1]
    span = devs * per

    def body(g, _):
        rows = pl.ds(pl.multiple_of(g * span, span), span)
        x = jnp.concatenate([src_ref[a, rows, :] for a in range(per)], axis=0).astype(BF16)
        y = dotf(pm_ref[...], x).reshape(devs, pad, c).astype(BF16)
        out_ref[pl.ds(pl.multiple_of(g * devs, devs), devs)] = y
        return 0
    lax.fori_loop(0, n // span, body, 0)


def unpack_rows(r_ref, pm_ref, store, devs, per, n):
    pad, c = r_ref.shape[1:]
    span = devs * per

    def body(g, _):
        x = r_ref[pl.ds(pl.multiple_of(g * devs, devs), devs)].reshape(devs * pad, c)
        y = dotf(pm_ref[...], x)
        rows = pl.ds(pl.multiple_of(g * span, span), span)
        for b in range(per):
            store(b, rows, y[b * span:(b + 1) * span])
        return 0
    lax.fori_loop(0, n // span, body, 0)


def local_bias(x_ref, wr_ref, b_ref):
    per = x_ref.shape[0]
    acc = None
    for r in range(per):
        t = dot_nt(wr_ref[r], ln(x_ref[r].astype(F32)))
        acc = t if acc is None else acc + t
    acc = acc.astype(BF16)
    for c in range(3):
        b_ref[c] = acc[:, c * b_ref.shape[2]:(c + 1) * b_ref.shape[2]]


def start_gather_kernel(x_ref, wr_ref, o_ref, b_ref, lsem, ssem, rsem):
    me = lax.axis_index('sp')
    local_bias(x_ref, wr_ref, b_ref)
    own = pltpu.make_async_copy(b_ref, o_ref.at[:, me], lsem)
    own.start()
    gather_start(me, b_ref, o_ref, ssem, rsem)
    own.wait()
    gather_rest(me, b_ref, o_ref, ssem, rsem)


def end_gather_kernel(n, devs, h_ref, pm_ref, wr_ref, x_ref, o_ref, r_ref, b_ref, lsem, ssem, rsem, esem):
    me = lax.axis_index('sp')
    own = pltpu.make_async_copy(h_ref.at[me], r_ref.at[me], lsem)
    own.start()
    exchange_start(me, h_ref, r_ref, n, ssem, esem)
    own.wait()
    exchange_wait(r_ref, n, ssem, esem)

    def store(b, rows, y):
        x_ref[b, rows, :] = y
    unpack_rows(r_ref, pm_ref, store, devs, x_ref.shape[0], x_ref.shape[1])
    local_bias(x_ref, wr_ref, b_ref)
    own = pltpu.make_async_copy(b_ref, o_ref.at[:, me], lsem)
    own.start()
    gather_start(me, b_ref, o_ref, ssem, rsem)
    own.wait()
    gather_rest(me, b_ref, o_ref, ssem, rsem)


def finish_kernel(devs, r_ref, pm_ref, z_ref, y_ref):
    def store(b, rows, y):
        y_ref[b, rows, :] = z_ref[b, rows, :] + y
    unpack_rows(r_ref, pm_ref, store, devs, z_ref.shape[0], z_ref.shape[1])


def attn_kernel(end, heads, nq, bdevs, pdevs, x_ref, gb_ref, wqvg_ref, wkT_ref, wo_ref, w1_ref, w2_ref, bm_ref, pm_ref, *refs):
    if end:
        o_ref = None
        h_ref, bf_ref, q_ref, g_ref, kT_ref, v_ref, hs_ref = refs
    else:
        o_ref, h_ref, bf_ref, q_ref, g_ref, kT_ref, v_ref, hs_ref = refs
    n, c = x_ref.shape[1:]
    hd = c // heads
    i = pl.program_id(0)

    @pl.when(i == 0)
    def _():
        wid = gb_ref.shape[3]
        span = n // (gb_ref.shape[1] // bdevs)

        def unpack(g, _):
            rows = pl.ds(pl.multiple_of(g * span, span), span)
            for s in range(3):
                b = gb_ref[s, pl.ds(pl.multiple_of(g * bdevs, bdevs), bdevs)].reshape(heads * span, wid)
                f = dotf(bm_ref[...], b) * LOG2E
                for h in range(heads):
                    bf_ref[h, rows, s * wid:(s + 1) * wid] = f[h * span:(h + 1) * span]
            return 0
        lax.fori_loop(0, n // span, unpack, 0)
        v_ref[:, c:] = jnp.ones((n, c), BF16)

    u = ln(x_ref[0].astype(F32))
    kT_ref[...] = dot_nt(wkT_ref[...], u).astype(BF16)
    pr = dotf(u, wqvg_ref[...])
    q_ref[...] = pr[:, :c].astype(BF16)
    v_ref[:, :c] = pr[:, c:2 * c].astype(BF16)
    g_ref[...] = jax.nn.sigmoid(pr[:, 2 * c:])
    scale = hd ** -0.5 * LOG2E

    def block(b, _):
        rows = pl.ds(pl.multiple_of(b * nq, nq), nq)
        qb = q_ref[rows, :]
        lane = lax.broadcasted_iota(jnp.int32, (nq, c), 1) // hd
        res = jnp.zeros((nq, c), F32)
        for h in range(heads):
            qm = jnp.where(lane == h, qb, jnp.zeros_like(qb))
            s = dotf(qm, kT_ref[...])
            t = s * scale + bf_ref[h, rows, :]
            m = jnp.max(t, axis=-1, keepdims=True)
            p = jnp.exp2(t - m).astype(BF16)
            o = dotf(p, v_ref[...])
            res = jnp.where(lane == h, o[:, :c] / o[:, c:], res)
        og = (res * g_ref[rows, :]).astype(BF16)
        upd = dotf(og, wo_ref[...])
        two = x_ref[0, rows, :].astype(F32) + upd
        if end:
            hid = jnp.maximum(dotf(ln(two), w1_ref[...]), 0).astype(BF16)
            hs_ref[i, rows, :] = upd + dotf(hid, w2_ref[...])
        else:
            o_ref[0, rows, :] = two
            hs_ref[i, rows, :] = two
        return 0
    lax.fori_loop(0, n // nq, block, 0)

    @pl.when(i == pl.num_programs(0) - 1)
    def _():
        pack_rows(hs_ref, pm_ref, h_ref, pdevs)


def attention(x, gb, wqkvg, wo, w1, w2, bm, pm, end, heads, bdevs, pdevs, nq):
    per, n, c = x.shape
    devs = gb.shape[1]
    pad = pm.shape[0] // pdevs
    wqvg = jnp.concatenate([wqkvg[:, :c], wqkvg[:, 2 * c:]], axis=1)
    wkT = wqkvg[:, c:2 * c].T
    full = lambda a: pl.BlockSpec(a.shape, lambda i: (0,) * a.ndim, pipeline_mode=pl.Buffered(1))
    row = pl.BlockSpec((1, n, c), lambda i: (i, 0, 0))
    packed = jax.ShapeDtypeStruct((devs, pad, c), BF16)
    outs = [] if end else [(row, jax.ShapeDtypeStruct((per, n, c), F32))]
    outs.append((full(packed), packed))
    return pl.pallas_call(
        functools.partial(attn_kernel, end, heads, nq, bdevs, pdevs),
        grid=(per,),
        in_specs=[row] + [full(a) for a in (gb, wqvg, wkT, wo, w1, w2, bm, pm)],
        out_specs=[o[0] for o in outs],
        out_shape=[o[1] for o in outs],
        scratch_shapes=[pltpu.VMEM((heads, n, n), F32), pltpu.VMEM((n, c), BF16), pltpu.VMEM((n, c), F32),
                        pltpu.VMEM((c, n), BF16), pltpu.VMEM((n, 2 * c), BF16), pltpu.VMEM((per, n, c), F32)],
        compiler_params=pltpu.CompilerParams(vmem_limit_bytes=56 * 2**20),
        name='attend_end' if end else 'attend_start',
    )(x, gb, wqvg, wkT, wo, w1, w2, bm, pm)


def solution(mesh):
    devs = mesh.shape['sp']
    row_spec = P(('dp', 'sp'), None, None)
    vmem = pl.BlockSpec(memory_space=pltpu.VMEM)
    hbm = pl.BlockSpec(memory_space=pl.ANY)
    params = pltpu.CompilerParams(has_side_effects=True, vmem_limit_bytes=32 * 2**20)
    dma = pltpu.SemaphoreType.DMA

    def local_fn(z, wqkvg_s, wb_s, wo_s, wqkvg_e, wb_e, wo_e, w1, w2):
        per, n, c = z.shape
        heads = wb_s.shape[0]
        bdevs, pdevs = 8, 4
        pad = -(-per * per // 8) * 8
        wid = n // 3
        nb = per * heads
        eye = jnp.eye(per, dtype=BF16)
        expand = lambda wb: (eye[:, :, None, None] * wb[None, None]).reshape(per, nb, c)
        bm = bias_matrix(per, heads, bdevs)
        pm = pack_matrix(per, pad, pdevs)
        um = unpack_matrix(per, pad, pdevs)
        gathered = jax.ShapeDtypeStruct((3, devs, nb, wid), BF16)
        gb = pl.pallas_call(
            start_gather_kernel, in_specs=[vmem] * 2, out_specs=hbm, out_shape=gathered,
            scratch_shapes=[pltpu.VMEM((3, nb, wid), BF16), dma, dma, dma((3, 6))],
            compiler_params=params, name='gather_start')(z, expand(wb_s))
        z1, hbuf = attention(z, gb, wqkvg_s, wo_s, w1, w2, bm, pm, False, heads, bdevs, pdevs, n)
        cols, gb = pl.pallas_call(
            functools.partial(end_gather_kernel, devs, pdevs), in_specs=[hbm, vmem, vmem], out_specs=[vmem, hbm],
            out_shape=[jax.ShapeDtypeStruct((per, n, c), F32), gathered],
            scratch_shapes=[pltpu.VMEM((devs, pad, c), BF16), pltpu.VMEM((3, nb, wid), BF16), dma, dma, dma((3, 6)), dma],
            compiler_params=params, name='gather_end')(hbuf, um, expand(wb_e))
        dbuf, = attention(cols, gb, wqkvg_e, wo_e, w1, w2, bm, pm, True, heads, bdevs, pdevs, n)
        rbuf = all_to_all(dbuf, devs)
        return pl.pallas_call(
            functools.partial(finish_kernel, pdevs), in_specs=[vmem] * 3, out_specs=vmem,
            out_shape=jax.ShapeDtypeStruct(z.shape, F32), compiler_params=pltpu.CompilerParams(vmem_limit_bytes=32 * 2**20), name='finish')(rbuf, um, z1)

    return jax.shard_map(local_fn, mesh=mesh, in_specs=(row_spec,) + (P(),) * 8, out_specs=row_spec, check_vma=False)
```

time: 326 us -> 220 us (0.67)
  Pallas kernels: 75 us -> 206 us
  waiting for transfers between devices: 131 us -> 0 us
  blocking collectives: 61.3 us -> 0 us
  between operations: 13.6 us -> 0.12 us
  other arithmetic: 13.9 us -> 1.4 us
  local copies, waits for them, and re-layouts: 25 us -> 12.9 us
  matrix products: 5.38 us -> 0 us
    all_gather x2 -> x0, waiting for transfers between devices: 131 us -> none  [the longest x1 69.4 us: local_fn(): bias_s = lax.all_gather(bias_s, 'sp', axis=1, tiled=True)]
    pallas_call x2 -> x6, Pallas kernels: 75 us -> 206 us  [the longest x2 81.1 us: attention(): pl.pallas_call(functools.partial(attn_kernel, end, heads, nq, bdevs, pdev...]
    all_to_all x2 -> x0, blocking collectives: 61.3 us -> none  [the longest x1 30.8 us: local_fn(): delta = lax.all_to_all(jnp.swapaxes(delta, 0, 1), 'sp', 0, 1, tiled=True)]
    convert_element_type x4 -> x0, local copies, waits for them, and re-layouts: 10.5 us -> none  [the longest x3 9.67 us: local_fn(): return z1 + delta.astype(F32)]
    all_gather x2 -> x0, local copies, waits for them, and re-layouts: 10.2 us -> none  [the longest x1 5.1 us: local_fn(): bias_s = lax.all_gather(bias_s, 'sp', axis=1, tiled=True)]
    unnamed x16 -> x22, local copies, waits for them, and re-layouts: 1.46 us -> 11.4 us
    reduce_sum x4 -> x0, other arithmetic: 5.74 us -> none  [the longest x2 2.88 us: ln(): mu = jnp.mean(x, axis=-1, keepdims=True)]
    dot_general x2 -> x0, matrix products: 5.38 us -> none  [the longest x1 2.7 us: local_fn(): jnp.einsum('hc,jkc->hjk', wb_s, ln(z), preferred_element_type=F32)]
  transfers between devices with their start and end apart: 2 -> 0, of which waited for: 2 -> 0; matrix products, arithmetic and copies ran while one was open for 1% -> 0% of each run, Pallas kernels for 0% -> 0%
where the time goes in v2:
time: 220 us
  Pallas kernels  206 us (94%)
  local copies, waits for them, and re-layouts  12.9 us (6%)
    pallas_call x2, Pallas kernels, attention(): pl.pallas_call(functools.partial(attn_kernel, end, heads, nq, bdevs, pdev...  81.1 us
    pallas_call x1, Pallas kernels, local_fn(): pl.pallas_call(functools.partial(end_gather_kernel, devs, pdevs), in_spec...  54.2 us
    pallas_call x1, Pallas kernels, local_fn(): pl.pallas_call(start_gather_kernel, in_specs=[vmem] * 2, out_specs=hbm, o...  36.9 us
    pallas_call x1, Pallas kernels, all_to_all(): pl.pallas_call(functools.partial(a2a_kernel, n), in_specs=[anyspec], out_...  27.1 us
    unnamed x22, local copies, waits for them, and re-layouts  11.4 us
    pallas_call x1, Pallas kernels, local_fn(): pl.pallas_call(functools.partial(finish_kernel, pdevs), in_specs=[vmem] *...  6.59 us

profile of v2, /device:TPU:1, one launch (start us, length us, event | category | flops | bytes accessed | tf_op | source)
XLA Modules:
  0.0 220.3 jit_solution(15242886236915050233)
XLA Ops:
  0.0 0.1 copy.15
  0.1 0.7 mul.47
  0.8 0.7 mul.51
  1.5 0.1 broadcast_multiply_fusion
  1.6 0.0 copy-start.1
  1.6 1.7 copy-done.1
  3.2 0.0 copy-start.8
  3.2 0.0 slice-start
  3.2 36.9 %gather_start.1.gb_ref = bf16[3,128,24,256]{3,2,1,0:T(8,128)(2,1)S(1)} custom-call(f32[6,768,128]{2,1,0:T(8,128)S(1)} %copy-done.1, bf16[6,24,128]{2,1,0:T(8,128)(2,1)S(1)} %get-tuple-element.18.wr_ref), custom_call_target="tpu_custom_call" | custom-call | tf_op jit(solution)/shard_map/gather_start/pallas_call | solution.py:363
  40.1 0.0 copy-start
  40.1 2.1 copy-done
  42.2 0.0 copy-done.8
  42.3 0.0 slice-done
  42.3 0.7 pad_maximum_fusion.wqvg_ref
  42.9 0.7 copy.18
  43.6 0.0 copy-start.7
  43.6 0.0 copy-start.9
  43.7 0.0 slice-start.1
  43.7 38.8 %attend_start.1 = (f32[6,768,128]{2,1,0:T(8,128)}, bf16[128,40,128]{2,1,0:T(8,128)(2,1)}) custom-call(f32[6,768,128]{2,1,0:T(8,128)} %x_ref.3, bf16[3,128,24,256]{3,2,1,0:T(8,128)(2,1)} %copy-done, bf16[128,384]{1,0:T(8,128)(2,1)} %pad_maximum_fusion.wqvg_ref, bf16[128,128]{1,0:T(8,128)(2,1)} %bitcast.6, bf16[128,128]{1,0:T(8,128)(2,1)} %wo_ref.2, ...), custom_call_target="tpu_custom_call" | custom-call | tf_op jit(solution)/shard_map/attend_start/pallas_call | solution.py:329
  82.5 0.0 copy-done.7
  82.5 0.0 copy-start.6
  82.5 1.3 copy-done.6
  83.8 54.2 %gather_end.1 = (f32[6,768,128]{2,1,0:T(8,128)S(1)}, bf16[3,128,24,256]{3,2,1,0:T(8,128)(2,1)S(1)}) custom-call(bf16[128,40,128]{2,1,0:T(8,128)(2,1)S(1)} %copy-done.6, bf16[144,160]{1,0:T(8,128)(2,1)S(1)} %copy-done.7, bf16[6,24,128]{2,1,0:T(8,128)(2,1)S(1)} %get-tuple-element.17.wr_ref), custom_call_target="tpu_custom_call" | custom-call | tf_op jit(solution)/shard_map/gather_end/pallas_call | solution.py:368
  138.0 0.0 copy-start.3
  138.0 2.1 copy-done.3
  140.1 0.0 copy-start.5
  140.1 1.4 copy-done.5
  141.6 0.0 copy-done.9
  141.6 0.0 slice-done.1
  141.6 0.6 pad_maximum_fusion.1.wqvg_ref
  142.2 0.7 copy.19
  142.9 42.3 %attend_end.1.h_ref = bf16[128,40,128]{2,1,0:T(8,128)(2,1)} custom-call(f32[6,768,128]{2,1,0:T(8,128)} %copy-done.5, bf16[3,128,24,256]{3,2,1,0:T(8,128)(2,1)} %copy-done.3, bf16[128,384]{1,0:T(8,128)(2,1)} %pad_maximum_fusion.1.wqvg_ref, bf16[128,128]{1,0:T(8,128)(2,1)} %bitcast.5, bf16[128,128]{1,0:T(8,128)(2,1)} %wo_ref.3, bf16[128,512]{1,0:T(8,128)(2,1)} %w1_ref.3, ...), custom_call_target="tpu_custom_call" | custom-call | tf_op jit(solution)/shard_map/attend_end/pallas_call | solution.py:329
  185.2 0.0 copy-start.4
  185.2 27.1 %exchange.1.r_ref = bf16[128,40,128]{2,1,0:T(8,128)(2,1)} custom-call(bf16[128,40,128]{2,1,0:T(8,128)(2,1)} %attend_end.1.h_ref), custom_call_target="tpu_custom_call" | custom-call | tf_op jit(solution)/shard_map/exchange/pallas_call | solution.py:119
  212.3 0.0 copy-done.4
  212.3 0.0 copy-start.2
  212.3 1.3 copy-done.2
  213.7 6.6 %finish.1 = f32[6,768,128]{2,1,0:T(8,128)} custom-call(bf16[128,40,128]{2,1,0:T(8,128)(2,1)S(1)} %copy-done.2, bf16[144,160]{1,0:T(8,128)(2,1)S(1)} %copy-done.7, f32[6,768,128]{2,1,0:T(8,128)S(1)} %copy-done.4), custom_call_target="tpu_custom_call" | custom-call | tf_op jit(solution)/shard_map/finish/pallas_call | solution.py:375
  (4 shorter events, 0.0 us)
Async XLA Ops:
  1.6 1.7 copy-start.1
  3.2 39.0 %copy-start.8 = (bf16[128,512]{1,0:T(8,128)(2,1)S(1)}, bf16[128,512]{1,0:T(8,128)(2,1)}, u32[]{:S(2)}) copy-start(bf16[128,512]{1,0:T(8,128)(2,1)} %param.13) | copy-start | bytes 393220
  3.2 39.0 %slice-start = ((bf16[128,512]{1,0:T(8,128)(2,1)}), bf16[128,256]{1,0:T(8,128)(2,1)S(1)}, s32[]{:S(2)}) async-start(bf16[128,512]{1,0:T(8,128)(2,1)} %param.13), calls=%async_computation | async-start | bytes 131072 | tf_op jit(solution)/shard_map/slice | solution.py:322
  40.1 2.1 copy-start
  43.6 38.8 %copy-start.7 = (bf16[144,160]{1,0:T(8,128)(2,1)S(1)}, bf16[144,160]{1,0:T(8,128)(2,1)}, u32[]{:S(2)}) copy-start(bf16[144,160]{1,0:T(8,128)(2,1)} %constant.8.clone.pm_ref) | copy-start | bytes 138244
  43.6 97.9 %copy-start.9 = (bf16[128,512]{1,0:T(8,128)(2,1)S(1)}, bf16[128,512]{1,0:T(8,128)(2,1)}, u32[]{:S(2)}) copy-start(bf16[128,512]{1,0:T(8,128)(2,1)} %param.16) | copy-start | bytes 393220
  43.7 97.9 %slice-start.1 = ((bf16[128,512]{1,0:T(8,128)(2,1)}), bf16[128,256]{1,0:T(8,128)(2,1)S(1)}, s32[]{:S(2)}) async-start(bf16[128,512]{1,0:T(8,128)(2,1)} %param.16), calls=%async_computation.1 | async-start | bytes 131072 | tf_op jit(solution)/shard_map/slice | solution.py:322
  82.5 1.3 copy-start.6
  138.0 2.1 copy-start.3
  140.1 1.4 copy-start.5
  185.2 27.1 %copy-start.4 = (f32[6,768,128]{2,1,0:T(8,128)S(1)}, f32[6,768,128]{2,1,0:T(8,128)}, u32[]{:S(2)}) copy-start(f32[6,768,128]{2,1,0:T(8,128)} %get-tuple-element.12.z_ref) | copy-start | bytes 7077892
  212.3 1.3 copy-start.2

commit v3 on v1

v3 whole, which is shorter than its diff:
```python
import functools
import math
import jax
import jax.numpy as jnp
import numpy as np
from jax import lax
from jax.experimental import pallas as pl
from jax.experimental.pallas import tpu as pltpu
from jax.sharding import PartitionSpec as P

F32, BF16 = jnp.float32, jnp.bfloat16
MESH = pl.DeviceIdType.MESH
LOG2E = math.log2(math.e)
EPS = 1e-5
X, Y, Z = 0, 1, 2
DEV = (2, 8, 32)
DIMS = ((X, Y, Z), (Y, Z, X), (Z, X, Y))
SLOT = ((2, 8, 32), (32, 1, 4), (2, 32, 8))
CORE = (1, 16, 1)


def ln(x):
    mu = jnp.mean(x, axis=-1, keepdims=True)
    c = x - mu
    var = jnp.mean(c * c, axis=-1, keepdims=True)
    return (c * lax.rsqrt(var + EPS)).astype(BF16)


def dotf(a, b):
    return jnp.dot(a, b, preferred_element_type=F32)


def dot_nt(a, b):
    return lax.dot_general(a, b, (((1,), (1,)), ((), ())), preferred_element_type=F32)


def mult(v, k):
    return pl.multiple_of(v, k)


def rcopy(src, dst, ssem, rsem, peer):
    return pltpu.make_async_remote_copy(src_ref=src, dst_ref=dst, send_sem=ssem, recv_sem=rsem, device_id={'sp': peer}, device_id_type=MESH)


def bytes_wait(ref, sem):
    pltpu.make_async_copy(ref, ref, sem).wait()


class Place:
    def __init__(self):
        self.me = lax.axis_index('sp')
        self.core = lax.rem(self.me, 2)
        self.at = [lax.rem(self.me // s, 4) for s in DEV]

    def ring(self, dim, t):
        return self.me + (lax.rem(self.at[dim] + t, 4) - self.at[dim]) * DEV[dim]

    def plane(self, c, t):
        return lax.rem(self.at[DIMS[c][2]] + t, 4)

    def slot(self, c, core=None, **over):
        at = [over.get('xyz'[d], self.at[d]) for d in range(3)]
        core = self.core if core is None else core
        return core * CORE[c] + sum(at[d] * SLOT[c][d] for d in range(3))


def slot_of(c, core, at):
    return core * CORE[c] + sum(at[d] * SLOT[c][d] for d in range(3))


def dest_of(c, plane, k):
    if c == 0:
        return plane * 32 + k
    if c == 1:
        return lax.rem(k, 16) * 8 + plane * 2 + k // 16
    return (k // 8) * 32 + plane * 8 + lax.rem(k, 8)


class Gather:
    def __init__(self, place, b_ref, g_ref, ssem, rsem):
        self.p, self.b, self.g, self.ssem, self.rsem = place, b_ref, g_ref, ssem, rsem

    def push(self, c, slot, peer, k):
        rcopy(self.g.at[c, slot], self.g.at[c, slot], self.ssem, self.rsem.at[c, k], peer).start()

    def first(self):
        p = self.p
        for c in range(3):
            slot = slot_of(c, p.core, p.at)
            for t in (1, 3, 2):
                rcopy(self.b.at[c], self.g.at[c, slot], self.ssem, self.rsem.at[c, 0], p.ring(DIMS[c][0], t)).start()
            rcopy(self.b.at[c], self.g.at[c, slot], self.ssem, self.rsem.at[c, 5], p.me ^ 1).start()
        for c in range(3):
            self.g[c, slot_of(c, p.core, p.at)] = self.b[c]

    def second(self):
        p = self.p
        for c in range(3):
            a, b, _ = DIMS[c]
            bytes_wait(self.g.at[c, pl.ds(0, 3)], self.rsem.at[c, 0])

            def body(j, _):
                at = list(p.at)
                at[a] = j
                slot = slot_of(c, p.core, at)
                own = j == p.at[a]

                @pl.when(own)
                def _():
                    for t in (1, 3, 2):
                        rcopy(self.b.at[c], self.g.at[c, slot], self.ssem, self.rsem.at[c, 1], p.ring(b, t)).start()

                @pl.when(jnp.logical_not(own))
                def _():
                    for t in (1, 3, 2):
                        self.push(c, slot, p.ring(b, t), 1)
                    self.push(c, slot, p.me ^ 1, 5)
                return 0
            lax.fori_loop(0, 4, body, 0)

    def third(self):
        p = self.p
        for c in range(3):
            a, b, d = DIMS[c]
            bytes_wait(self.g.at[c, pl.ds(0, 12)], self.rsem.at[c, 1])

            def body(j, _):
                at = list(p.at)
                at[a] = lax.rem(j, 4)
                at[b] = j // 4
                slot = slot_of(c, p.core, at)
                self.push(c, slot, p.ring(d, 1), 2)
                self.push(c, slot, p.ring(d, 3), 3)

                @pl.when(at[b] != p.at[b])
                def _():
                    self.push(c, slot, p.me ^ 1, 5)
                return 0
            lax.fori_loop(0, 16, body, 0)

    def plane_body(self, c, t, fn):
        p = self.p
        a, b, d = DIMS[c]

        def body(j, _):
            at = list(p.at)
            at[a] = lax.rem(j, 4)
            at[b] = j // 4
            at[d] = lax.rem(p.at[d] + t, 4)
            fn(j, slot_of(c, p.core, at))
            return 0
        lax.fori_loop(0, 16, body, 0)

    def forward(self):
        p = self.p
        for side in range(2):
            for c in range(3):
                bytes_wait(self.g.at[c, pl.ds(0, 16)], self.rsem.at[c, 2 + side])
                to = p.ring(DIMS[c][2], 1 if side == 0 else 3)

                def fn(j, slot):
                    @pl.when(j // 8 == side)
                    def _():
                        self.push(c, slot, to, 4)
                    self.push(c, slot, p.me ^ 1, 6 + side)
                self.plane_body(c, 3 if side == 0 else 1, fn)

    def last(self):
        for c in range(3):
            bytes_wait(self.g.at[c, pl.ds(0, 16)], self.rsem.at[c, 4])
            self.plane_body(c, 2, lambda j, slot: self.push(c, slot, self.p.me ^ 1, 8))

    def partner_wait(self, k):
        for c in range(3):
            bytes_wait(self.g.at[c, pl.ds(0, 16)], self.rsem.at[c, k])

    def drain(self):
        for c in range(3):
            bytes_wait(self.g.at[c, pl.ds(0, 127)], self.ssem)


def load_rows(z_ref, xc_ref):
    def body(i, _):
        for r2 in range(2):
            v = z_ref[i, pl.ds(r2, 128, stride=6), :]
            for p in range(4):
                xc_ref[i, pl.ds(p * 64 + r2 * 32, 32), :] = v[p * 32:(p + 1) * 32]
            for x in range(4):
                for core in range(2):
                    xc_ref[i, pl.ds(256 + x * 64 + r2 * 32 + core * 16, 16), :] = z_ref[i, pl.ds((x * 2 + core) * 6 + 2 + r2, 16, stride=48), :]
            for y in range(4):
                for zz in range(4):
                    xc_ref[i, pl.ds(512 + y * 64 + r2 * 32 + zz * 8, 8), :] = z_ref[i, pl.ds((zz * 32 + y * 8) * 6 + 4 + r2, 8, stride=6), :]
        return 0
    lax.fori_loop(0, z_ref.shape[0], body, 0)


def store_rows(place, y_ref, hb_ref, t):
    def body(i, _):
        for r2 in range(2):
            p0, p1, p2 = (place.plane(c, t) for c in range(3))
            y_ref[i, pl.ds(p0 * 192 + r2, 32, stride=6), :] = hb_ref[i, pl.ds(r2 * 32, 32), :]
            for core in range(2):
                y_ref[i, pl.ds(p1 * 12 + core * 6 + 2 + r2, 16, stride=48), :] = hb_ref[i, pl.ds(64 + r2 * 32 + core * 16, 16), :]
            for zz in range(4):
                y_ref[i, pl.ds(p2 * 48 + zz * 192 + 4 + r2, 8, stride=6), :] = hb_ref[i, pl.ds(128 + r2 * 32 + zz * 8, 8), :]
        return 0
    lax.fori_loop(0, y_ref.shape[0], body, 0)


def receive_rows(rb_ref, um_ref, xc_ref):
    for c in range(3):
        def body(g, _):
            zz, y = g // 4, lax.rem(g, 4)
            x = rb_ref[c, pl.ds(mult(g * 8, 8), 8)].reshape(128, 128)
            f = dotf(um_ref[...], x)
            for b in range(2):
                for r in range(6):
                    v = f[(b * 6 + r) * 8:(b * 6 + r + 1) * 8]
                    r2 = r % 2
                    if r // 2 == 0:
                        xc_ref[2 * c + b, pl.ds(mult(zz * 64 + r2 * 32 + y * 8, 8), 8), :] = v
                    elif r // 2 == 2:
                        xc_ref[2 * c + b, pl.ds(mult(512 + y * 64 + r2 * 32 + zz * 8, 8), 8), :] = v
                    else:
                        for core in range(2):
                            xc_ref[2 * c + b, pl.ds(256 + r2 * 32 + core * 16 + g, 4, stride=64), :] = v[core * 4:core * 4 + 4]
            return 0
        lax.fori_loop(0, 16, body, 0)


def finish_rows(rb_ref, um_ref, y_ref):
    for c in range(3):
        def body(g, _):
            x = rb_ref[c, pl.ds(mult(g * 8, 8), 8)].reshape(128, 128)
            f = dotf(um_ref[...], x)
            for b in range(2):
                for r in range(6):
                    at = pl.ds(g * 48 + r, 8, stride=6)
                    y_ref[2 * c + b, at, :] = y_ref[2 * c + b, at, :] + f[(b * 6 + r) * 8:(b * 6 + r + 1) * 8]
            return 0
        lax.fori_loop(0, 16, body, 0)


def stage(end, place, gather, heads, xc_ref, b_ref, gb_ref, w_ref, wb_ref, wo_ref, w1_ref, w2_ref, bm_ref, pm_ref, y_ref, rb_ref, esem, fsem,
          u_ref, q_ref, g_ref, kT_ref, v_ref, bf_ref, hb_ref, sb_ref):
    per, n, c = xc_ref.shape
    hd = c // heads
    nq = n // 4
    scale = hd ** -0.5 * LOG2E
    me = place.me

    for col in range(3):
        acc = None
        for r2 in range(2):
            i = col * 2 + r2
            u = ln(xc_ref[i])
            u_ref[i] = u
            t = dot_nt(wb_ref[r2], u)
            acc = t if acc is None else acc + t
        b_ref[col] = acc.astype(BF16)
    gather.first()

    wkT = w_ref[:, c:2 * c].T

    def project(i, _):
        u = u_ref[i]
        kT_ref[i] = dot_nt(wkT, u).astype(BF16)
        q_ref[i] = dotf(u, w_ref[:, :c]).astype(BF16)
        vg = dotf(u, w_ref[:, 2 * c:])
        v_ref[i, :, :c] = vg[:, :c].astype(BF16)
        v_ref[i, :, c:] = jnp.ones((n, c), BF16)
        g_ref[i] = jax.nn.sigmoid(vg[:, c:])
        return 0

    lax.fori_loop(0, per // 2, project, 0)
    gather.second()
    lax.fori_loop(per // 2, per, project, 0)
    gather.third()

    def block(step, _):
        t = jnp.where(step == 1, 3, jnp.where(step == 2, 1, jnp.where(step == 3, 2, 0)))
        for k, sem in ((0, 5), (1, 6), (2, 7), (3, 8)):
            @pl.when(step == k)
            def _():
                gather.partner_wait(sem)
        planes = [place.plane(col, t) for col in range(3)]
        for col in range(3):
            b = gb_ref[col, pl.ds(mult(planes[col] * 32, 32), 32)].reshape(256, n)
            f = dotf(bm_ref[...], b) * LOG2E
            for h in range(heads):
                bf_ref[h, col * 64:(col + 1) * 64, :] = f[h * 64:(h + 1) * 64]
        rows = [pl.ds(mult(col * 256 + planes[col] * 64, 64), 64) for col in range(3)]

        def row(i, _):
            @pl.when(jnp.logical_and(step == 0, i == 3))
            def _():
                gather.forward()

            @pl.when(jnp.logical_and(step == 1, i == 3))
            def _():
                gather.last()
            qb = jnp.concatenate([q_ref[i, r, :] for r in rows], axis=0)
            lane = lax.broadcasted_iota(jnp.int32, (nq, c), 1) // hd
            res = jnp.zeros((nq, c), F32)
            for h in range(heads):
                qm = jnp.where(lane == h, qb, jnp.zeros_like(qb))
                s = dotf(qm, kT_ref[i])
                s = s * scale + bf_ref[h]
                m = jnp.max(s, axis=-1, keepdims=True)
                p = jnp.exp2(s - m).astype(BF16)
                o = dotf(p, v_ref[i])
                res = jnp.where(lane == h, o[:, :c] / o[:, c:], res)
            og = (res * jnp.concatenate([g_ref[i, r, :] for r in rows], axis=0)).astype(BF16)
            upd = dotf(og, wo_ref[...])
            if end:
                hb_ref[i] = upd
            else:
                hb_ref[i] = jnp.concatenate([xc_ref[i, r, :] for r in rows], axis=0) + upd
            return 0
        lax.fori_loop(0, per, row, 0)

        if end:
            def trans(i, _):
                upd = jnp.concatenate([hb_ref[2 * i], hb_ref[2 * i + 1]], axis=0)
                two = jnp.concatenate([xc_ref[2 * i + a, r, :] for a in range(2) for r in rows], axis=0) + upd
                hid = jnp.maximum(dotf(ln(two), w1_ref[...]), 0).astype(BF16)
                new = upd + dotf(hid, w2_ref[...])
                hb_ref[2 * i] = new[:nq]
                hb_ref[2 * i + 1] = new[nq:]
                return 0
            lax.fori_loop(0, per // 2, trans, 0)
        else:
            store_rows(place, y_ref, hb_ref, t)

        def pack(kg, _):
            for col in range(3):
                x = jnp.concatenate([hb_ref[i, pl.ds(mult(col * 64 + r2 * 32 + kg * 8, 8), 8), :] for i in range(per) for r2 in range(2)], axis=0)
                f = dotf(pm_ref[...], x.astype(BF16)).reshape(8, 16, c).astype(BF16)
                sb_ref[col, pl.ds(mult(planes[col] * 32 + kg * 8, 8), 8)] = f
            return 0
        lax.fori_loop(0, 4, pack, 0)

        def send(k, _):
            for col in range(3):
                slot = planes[col] * 32 + k
                d = dest_of(col, planes[col], k)

                @pl.when(d != me)
                def _():
                    rcopy(sb_ref.at[col, slot], rb_ref.at[col, me], fsem, esem, d).start()
            return 0
        lax.fori_loop(0, 32, send, 0)
        return 0
    lax.fori_loop(0, 4, block, 0)
    for col in range(3):
        rb_ref[col, me] = sb_ref[col, slot_of(col, place.core, place.at)]
    gather.drain()
    bytes_wait(rb_ref.at[:, pl.ds(0, 127)], fsem)
    bytes_wait(rb_ref.at[:, pl.ds(0, 127)], esem)


def kernel(heads, z_ref, ws_ref, wos_ref, we_ref, woe_ref, w1_ref, w2_ref, wb_ref, bm_ref, pm_ref, um1_ref, um2_ref, y_ref,
           xc_ref, b_ref, gb1_ref, gb2_ref, rb1_ref, rb2_ref, u_ref, q_ref, g_ref, kT_ref, v_ref, bf_ref, hb_ref, sb_ref,
           gs1, gr1, gs2, gr2, e1, f1, e2, f2):
    place = Place()
    work = (u_ref, q_ref, g_ref, kT_ref, v_ref, bf_ref, hb_ref, sb_ref)
    load_rows(z_ref, xc_ref)
    stage(False, place, Gather(place, b_ref.at[0], gb1_ref, gs1, gr1), heads, xc_ref, b_ref.at[0], gb1_ref, ws_ref, wb_ref.at[0], wos_ref, w1_ref, w2_ref,
          bm_ref, pm_ref, y_ref, rb1_ref, e1, f1, *work)
    receive_rows(rb1_ref, um1_ref, xc_ref)
    stage(True, place, Gather(place, b_ref.at[1], gb2_ref, gs2, gr2), heads, xc_ref, b_ref.at[1], gb2_ref, we_ref, wb_ref.at[1], woe_ref, w1_ref, w2_ref,
          bm_ref, pm_ref, y_ref, rb2_ref, e2, f2, *work)
    finish_rows(rb2_ref, um2_ref, y_ref)


def pack_matrix():
    m = np.zeros((8, 16, 6, 2, 8), np.float32)
    for k in range(8):
        for i in range(6):
            for r in range(2):
                m[k, i * 2 + r, i, r, k] = 1
    return jnp.asarray(m.reshape(128, 96), BF16)


def unpack_matrix(swap):
    m = np.zeros((2, 6, 8, 8, 16), np.float32)
    for k in range(8):
        for i in range(6):
            for r in range(2):
                row = (k % 2) * 4 + k // 2 if swap and i // 2 == 1 else k
                m[r, i, row, k, i * 2 + r] = 1
    return jnp.asarray(m.reshape(96, 128), BF16)


def bias_matrix(heads):
    m = np.zeros((heads, 2, 32, 32, 2, heads), np.float32)
    for k in range(32):
        for r in range(2):
            for h in range(heads):
                m[h, r, k, k, r, h] = 1
    return jnp.asarray(m.reshape(256, 256), BF16)


def solution(mesh):
    devs = mesh.shape['sp']
    row_spec = P(('dp', 'sp'), None, None)
    vmem = pl.BlockSpec(memory_space=pltpu.VMEM)
    dma = pltpu.SemaphoreType.DMA

    def local_fn(z, wqkvg_s, wb_s, wo_s, wqkvg_e, wb_e, wo_e, w1, w2):
        per, n, c = z.shape
        heads = wb_s.shape[0]
        wb = jnp.stack([wb_s, wb_e])
        none = jnp.zeros_like(wb)
        wb = jnp.stack([jnp.concatenate([wb, none], 1), jnp.concatenate([none, wb], 1)], 1)
        args = (z, wqkvg_s, wo_s, wqkvg_e, wo_e, w1, w2, wb, bias_matrix(heads), pack_matrix(), unpack_matrix(True), unpack_matrix(False))
        return pl.pallas_call(
            functools.partial(kernel, heads), in_specs=[vmem] * len(args), out_specs=vmem,
            out_shape=jax.ShapeDtypeStruct(z.shape, F32),
            scratch_shapes=[
                pltpu.VMEM((per, n, c), F32), pltpu.VMEM((2, 3, 8, n), BF16),
                pltpu.VMEM((3, devs, 8, n), BF16), pltpu.VMEM((3, devs, 8, n), BF16),
                pltpu.VMEM((3, devs, 16, c), BF16), pltpu.VMEM((3, devs, 16, c), BF16),
                pltpu.VMEM((per, n, c), BF16), pltpu.VMEM((per, n, c), BF16), pltpu.VMEM((per, n, c), F32),
                pltpu.VMEM((per, c, n), BF16), pltpu.VMEM((per, n, 2 * c), BF16), pltpu.VMEM((heads, n // 4, n), F32),
                pltpu.VMEM((per, n // 4, c), F32), pltpu.VMEM((3, devs, 16, c), BF16),
                dma, dma((3, 9)), dma, dma((3, 9)), dma, dma, dma, dma],
            compiler_params=pltpu.CompilerParams(has_side_effects=True, vmem_limit_bytes=60 * 2**20), name='block')(*args)

    return jax.shard_map(local_fn, mesh=mesh, in_specs=(row_spec,) + (P(),) * 8, out_specs=row_spec, check_vma=False)
```

time: 326 us -> 172 us (0.53)
  waiting for transfers between devices: 131 us -> 0 us
  Pallas kernels: 75 us -> 168 us
  blocking collectives: 61.3 us -> 0 us
  local copies, waits for them, and re-layouts: 25 us -> 3.23 us
  between operations: 13.6 us -> 0.01 us
  other arithmetic: 13.9 us -> 1.31 us
  matrix products: 5.38 us -> 0 us
    all_gather x2 -> x0, waiting for transfers between devices: 131 us -> none  [the longest x1 69.4 us: local_fn(): bias_s = lax.all_gather(bias_s, 'sp', axis=1, tiled=True)]
    pallas_call x2 -> x1, Pallas kernels: 75 us -> 168 us  [local_fn(): pl.pallas_call(functools.partial(kernel, heads), in_specs=[vmem] * len(ar...]
    all_to_all x2 -> x0, blocking collectives: 61.3 us -> none  [the longest x1 30.8 us: local_fn(): delta = lax.all_to_all(jnp.swapaxes(delta, 0, 1), 'sp', 0, 1, tiled=True)]
    convert_element_type x4 -> x0, local copies, waits for them, and re-layouts: 10.5 us -> none  [the longest x3 9.67 us: local_fn(): return z1 + delta.astype(F32)]
    all_gather x2 -> x0, local copies, waits for them, and re-layouts: 10.2 us -> none  [the longest x1 5.1 us: local_fn(): bias_s = lax.all_gather(bias_s, 'sp', axis=1, tiled=True)]
    reduce_sum x4 -> x0, other arithmetic: 5.74 us -> none  [the longest x2 2.88 us: ln(): mu = jnp.mean(x, axis=-1, keepdims=True)]
    dot_general x2 -> x0, matrix products: 5.38 us -> none  [the longest x1 2.7 us: local_fn(): jnp.einsum('hc,jkc->hjk', wb_s, ln(z), preferred_element_type=F32)]
    add x1 -> x0, other arithmetic: 3.47 us -> none  [local_fn(): return z1 + delta.astype(F32)]
  transfers between devices with their start and end apart: 2 -> 0, of which waited for: 2 -> 0; matrix products, arithmetic and copies ran while one was open for 1% -> 0% of each run, Pallas kernels for 0% -> 0%
where the time goes in v3:
time: 172 us
  Pallas kernels  168 us (98%)
  local copies, waits for them, and re-layouts  3.23 us (2%)
    pallas_call x1, Pallas kernels, local_fn(): pl.pallas_call(functools.partial(kernel, heads), in_specs=[vmem] * len(ar...  168 us

profile of v3, /device:TPU:1, one launch (start us, length us, event | category | flops | bytes accessed | tf_op | source)
XLA Modules:
  0.0 172.3 jit_solution(760790331923653858)
XLA Ops:
  0.0 0.7 pad_maximum_fusion.1
  0.7 0.6 pad_maximum_fusion.wb_ref
  1.3 167.7 %block.1 = f32[6,768,128]{2,1,0:T(8,128)} custom-call(f32[6,768,128]{2,1,0:T(8,128)} %z_ref.1, bf16[128,512]{1,0:T(8,128)(2,1)} %ws_ref.1, bf16[128,128]{1,0:T(8,128)(2,1)} %wos_ref.1, bf16[128,512]{1,0:T(8,128)(2,1)} %we_ref.1, bf16[128,128]{1,0:T(8,128)(2,1)} %woe_ref.1, bf16[128,512]{1,0:T(8,128)(2,1)} %w1_ref.1, bf16[512,128]{1,0:T(8,128)(2,1)} %w2_ref.1, ...), custom_call_target="tpu_custom_call" | custom-call | tf_op jit(solution)/shard_map/block/pallas_call | solution.py:418
  169.1 3.2 %copy.16 = f32[6,768,128]{2,1,0:T(8,128)} copy(f32[6,768,128]{2,1,0:T(8,128)} %block.1) | data formatting | bytes 4718592
  (1 shorter events, 0.0 us)

commit v4 on v3

v4 whole, which is shorter than its diff:
```python
import functools
import math
import jax
import jax.numpy as jnp
import numpy as np
from jax import lax
from jax.experimental import pallas as pl
from jax.experimental.pallas import tpu as pltpu
from jax.sharding import PartitionSpec as P

F32, BF16 = jnp.float32, jnp.bfloat16
MESH = pl.DeviceIdType.MESH
LOG2E = math.log2(math.e)
EPS = 1e-5
X, Y, Z = 0, 1, 2
DEV = (2, 8, 32)
DIMS = ((X, Y, Z), (Y, Z, X), (Z, X, Y))
SLOT = ((1, 4, 32), (32, 1, 4), (4, 32, 1))


def ln(x):
    mu = jnp.mean(x, axis=-1, keepdims=True)
    c = x - mu
    var = jnp.mean(c * c, axis=-1, keepdims=True)
    return (c * lax.rsqrt(var + EPS)).astype(BF16)


def dotf(a, b):
    return jnp.dot(a, b, preferred_element_type=F32)


def dot_nt(a, b):
    return lax.dot_general(a, b, (((1,), (1,)), ((), ())), preferred_element_type=F32)


def mult(v, k):
    return pl.multiple_of(v, k)


def rcopy(src, dst, ssem, rsem, peer):
    return pltpu.make_async_remote_copy(src_ref=src, dst_ref=dst, send_sem=ssem, recv_sem=rsem, device_id={'sp': peer}, device_id_type=MESH)


def bytes_wait(ref, sem):
    pltpu.make_async_copy(ref, ref, sem).wait()


class Place:
    def __init__(self):
        self.me = lax.axis_index('sp')
        self.core = lax.rem(self.me, 2)
        self.at = [lax.rem(self.me // s, 4) for s in DEV]

    def ring(self, dim, t):
        return self.me + (lax.rem(self.at[dim] + t, 4) - self.at[dim]) * DEV[dim]

    def plane(self, c, t):
        return lax.rem(self.at[DIMS[c][2]] + t, 4)


def slot_of(c, place):
    return place.core * 16 + sum(place.at[d] * SLOT[c][d] for d in range(3))


def dest_of(c, plane, k):
    if c == 0:
        return plane * 32 + lax.rem(k, 16) * 2 + k // 16
    if c == 1:
        return lax.rem(k, 16) * 8 + plane * 2 + k // 16
    return lax.rem(k, 4) * 32 + plane * 8 + lax.rem(k // 4, 4) * 2 + k // 16


class Gather:
    def __init__(self, place, b_ref, g_ref, ssem, rsem):
        self.p, self.b, self.g, self.ssem, self.rsem = place, b_ref, g_ref, ssem, rsem

    def push(self, c, start, count, peer, k):
        part = self.g.at[c, pl.ds(start, count)]
        rcopy(part, part, self.ssem, self.rsem.at[c, k], peer).start()

    def half(self, c, t):
        return self.p.plane(c, t) * 32 + self.p.core * 16

    def first(self):
        p = self.p
        for c in range(3):
            slot = slot_of(c, p)
            for t in (1, 3, 2):
                rcopy(self.b.at[c], self.g.at[c, slot], self.ssem, self.rsem.at[c, 0], p.ring(DIMS[c][0], t)).start()
        for c in range(3):
            self.g[c, slot_of(c, p)] = self.b[c]

    def second(self):
        p = self.p
        for c in range(3):
            b = DIMS[c][1]
            bytes_wait(self.g.at[c, pl.ds(0, 3)], self.rsem.at[c, 0])
            for t in (1, 3, 2):
                self.push(c, self.half(c, 0) + p.at[b] * 4, 4, p.ring(b, t), 1)

    def third(self):
        p = self.p
        for c in range(3):
            d = DIMS[c][2]
            bytes_wait(self.g.at[c, pl.ds(0, 12)], self.rsem.at[c, 1])
            self.push(c, self.half(c, 0), 16, p.me ^ 1, 5)
            self.push(c, self.half(c, 0), 16, p.ring(d, 1), 2)
            self.push(c, self.half(c, 0), 16, p.ring(d, 3), 3)

    def forward(self):
        p = self.p
        for side, t in ((0, 3), (1, 1)):
            for c in range(3):
                bytes_wait(self.g.at[c, pl.ds(0, 16)], self.rsem.at[c, 2 + side])
                self.push(c, self.half(c, t), 16, p.me ^ 1, 6 + side)
                self.push(c, self.half(c, t) + side * 8, 8, p.ring(DIMS[c][2], 4 - t), 4)

    def last(self):
        for c in range(3):
            bytes_wait(self.g.at[c, pl.ds(0, 16)], self.rsem.at[c, 4])
            self.push(c, self.half(c, 2), 16, self.p.me ^ 1, 8)

    def partner_wait(self, k):
        for c in range(3):
            bytes_wait(self.g.at[c, pl.ds(0, 16)], self.rsem.at[c, k])

    def drain(self):
        for c in range(3):
            bytes_wait(self.g.at[c, pl.ds(0, 127)], self.ssem)


def load_rows(z_ref, xc_ref):
    def body(i, _):
        for r2 in range(2):
            for p in range(4):
                for core in range(2):
                    at = p * 64 + r2 * 32 + core * 16
                    xc_ref[i, pl.ds(at, 16), :] = z_ref[i, pl.ds((p * 32 + core) * 6 + r2, 16, stride=12), :]
                    xc_ref[i, pl.ds(256 + at, 16), :] = z_ref[i, pl.ds((p * 2 + core) * 6 + 2 + r2, 16, stride=48), :]
                    for x in range(4):
                        xc_ref[i, pl.ds(512 + at + x * 4, 4), :] = z_ref[i, pl.ds((p * 8 + x * 2 + core) * 6 + 4 + r2, 4, stride=192), :]
        return 0
    lax.fori_loop(0, z_ref.shape[0], body, 0)


def store_rows(place, y_ref, hb_ref, t):
    def body(i, _):
        p0, p1, p2 = (place.plane(c, t) for c in range(3))
        for r2 in range(2):
            for core in range(2):
                at = r2 * 32 + core * 16
                y_ref[i, pl.ds(p0 * 192 + core * 6 + r2, 16, stride=12), :] = hb_ref[i, pl.ds(at, 16), :]
                y_ref[i, pl.ds(p1 * 12 + core * 6 + 2 + r2, 16, stride=48), :] = hb_ref[i, pl.ds(64 + at, 16), :]
                for x in range(4):
                    y_ref[i, pl.ds(p2 * 48 + x * 12 + core * 6 + 4 + r2, 4, stride=192), :] = hb_ref[i, pl.ds(128 + at + x * 4, 4), :]
        return 0
    lax.fori_loop(0, y_ref.shape[0], body, 0)


def receive_rows(rb_ref, um_ref, xc_ref):
    for c in range(3):
        def body(zz, _):
            for y in range(4):
                x = rb_ref[c, pl.ds(mult(zz * 32 + y * 8, 8), 8)].reshape(128, 128)
                f = dotf(um_ref[...], x)
                for b in range(2):
                    for r in range(6):
                        for core in range(2):
                            v = f[(b * 6 + r) * 8 + core * 4:(b * 6 + r) * 8 + core * 4 + 4]
                            at = (r % 2) * 32 + core * 16
                            if r // 2 == 0:
                                xc_ref[2 * c + b, pl.ds(mult(zz * 64, 64) + at + y * 4, 4), :] = v
                            elif r // 2 == 1:
                                xc_ref[2 * c + b, pl.ds(256 + at + zz * 4 + y, 4, stride=64), :] = v
                            else:
                                xc_ref[2 * c + b, pl.ds(512 + at + y * 64 + zz, 4, stride=4), :] = v
            return 0
        lax.fori_loop(0, 4, body, 0)


def finish_rows(rb_ref, um_ref, y_ref):
    for c in range(3):
        def body(g, _):
            x = rb_ref[c, pl.ds(mult(g * 8, 8), 8)].reshape(128, 128)
            f = dotf(um_ref[...], x)
            for b in range(2):
                for r in range(6):
                    at = pl.ds(g * 48 + r, 8, stride=6)
                    y_ref[2 * c + b, at, :] = y_ref[2 * c + b, at, :] + f[(b * 6 + r) * 8:(b * 6 + r + 1) * 8]
            return 0
        lax.fori_loop(0, 16, body, 0, unroll=4)


def stage(end, place, gather, heads, xc_ref, b_ref, gb_ref, w_ref, wb_ref, wo_ref, w1_ref, w2_ref, bm_ref, pm_ref, y_ref, rb_ref, esem, fsem,
          u_ref, q_ref, g_ref, kT_ref, v_ref, bf_ref, hb_ref, sb_ref, s_refs, p_refs):
    per, n, c = xc_ref.shape
    hd = c // heads
    nq = n // 4
    scale = hd ** -0.5 * LOG2E
    me = place.me

    for col in range(3):
        acc = None
        for r2 in range(2):
            i = col * 2 + r2
            u = ln(xc_ref[i])
            u_ref[i] = u
            t = dot_nt(wb_ref[r2], u)
            acc = t if acc is None else acc + t
        b_ref[col] = acc.astype(BF16)
    gather.first()

    wkT = w_ref[:, c:2 * c].T

    def project(i, _):
        u = u_ref[i]
        kT_ref[i] = dot_nt(wkT, u).astype(BF16)
        q_ref[i] = dotf(u, w_ref[:, :c]).astype(BF16)
        vg = dotf(u, w_ref[:, 2 * c:])
        v_ref[i, :, :c] = vg[:, :c].astype(BF16)
        v_ref[i, :, c:] = jnp.ones((n, c), BF16)
        g_ref[i] = jax.nn.sigmoid(vg[:, c:])
        return 0

    lax.fori_loop(0, per // 2, project, 0)
    gather.second()
    lax.fori_loop(per // 2, per, project, 0)
    gather.third()

    order = (0, 3, 1, 2)

    def pick(step):
        return jnp.where(step == 1, 3, jnp.where(step == 2, 1, jnp.where(step == 3, 2, 0)))

    def send(col, plane, o):
        k = lax.rem(slot_of(col, place), 32) ^ o
        rcopy(sb_ref.at[col, plane * 32 + k], rb_ref.at[col, me], fsem, esem, dest_of(col, plane, k)).start()

    def block(step, _):
        first = isinstance(step, int)
        t = 0 if first else pick(step)
        before = None if first else [place.plane(col, pick(step - 1)) for col in range(3)]
        gather.partner_wait(5 + step)
        planes = [place.plane(col, t) for col in range(3)]
        for col in range(3):
            b = gb_ref[col, pl.ds(mult(planes[col] * 32, 32), 32)].reshape(256, n)
            f = dotf(bm_ref[...], b) * LOG2E
            for h in range(heads):
                bf_ref[h * nq + col * 64:h * nq + (col + 1) * 64, :] = f[h * 64:(h + 1) * 64]
        rows = [pl.ds(mult(col * 256 + planes[col] * 64, 64), 64) for col in range(3)]

        lane = lax.broadcasted_iota(jnp.int32, (nq, c), 1) // hd

        def scores(i):
            qb = jnp.concatenate([q_ref[i, r, :] for r in rows], axis=0)
            qm = jnp.concatenate([jnp.where(lane == h, qb, jnp.zeros_like(qb)) for h in range(heads)], axis=0)
            s_refs[i % 2][...] = dotf(qm, kT_ref[i]) * scale + bf_ref[...]

        def soften(i):
            t = s_refs[i % 2][...]
            m = jnp.max(t, axis=-1, keepdims=True)
            p_refs[i % 2][...] = jnp.exp2(t - m).astype(BF16)

        def mix(i):
            o = dotf(p_refs[i % 2][...], v_ref[i])
            o = o[:, :c] / o[:, c:]
            res = jnp.zeros((nq, c), F32)
            for h in range(heads):
                res = jnp.where(lane == h, o[h * nq:(h + 1) * nq], res)
            og = (res * jnp.concatenate([g_ref[i, r, :] for r in rows], axis=0)).astype(BF16)
            upd = dotf(og, wo_ref[...])
            if end:
                hb_ref[i] = upd
            else:
                hb_ref[i] = jnp.concatenate([xc_ref[i, r, :] for r in rows], axis=0) + upd

        if not first:
            @pl.when(step > 1)
            def _():
                for col in range(3):
                    send(col, before[col], 0)
        scores(0)
        for i in range(per):
            if not first:
                for o in range(1 + i * 31 // per, 1 + (i + 1) * 31 // per):
                    for col in range(3):
                        send(col, before[col], o)
            if i + 1 < per:
                scores(i + 1)
            soften(i)
            if i > 0:
                mix(i - 1)
        mix(per - 1)
        if first:
            gather.forward()
        else:
            @pl.when(step == 1)
            def _():
                gather.last()

        if end:
            def trans(i, _):
                upd = jnp.concatenate([hb_ref[2 * i], hb_ref[2 * i + 1]], axis=0)
                two = jnp.concatenate([xc_ref[2 * i + a, r, :] for a in range(2) for r in rows], axis=0) + upd
                hid = jnp.maximum(dotf(ln(two), w1_ref[...]), 0).astype(BF16)
                new = upd + dotf(hid, w2_ref[...])
                hb_ref[2 * i] = new[:nq]
                hb_ref[2 * i + 1] = new[nq:]
                return 0
            lax.fori_loop(0, per // 2, trans, 0, unroll=3)
        else:
            store_rows(place, y_ref, hb_ref, t)

        def pack(kg, _):
            for col in range(3):
                x = jnp.concatenate([hb_ref[i, pl.ds(mult(col * 64 + r2 * 32 + kg * 8, 8), 8), :] for i in range(per) for r2 in range(2)], axis=0)
                f = dotf(pm_ref[...], x.astype(BF16)).reshape(8, 16, c).astype(BF16)
                sb_ref[col, pl.ds(mult(planes[col] * 32 + kg * 8, 8), 8)] = f
            return 0
        lax.fori_loop(0, 4, pack, 0, unroll=4)

        return 0

    block(0, 0)
    lax.fori_loop(1, 4, block, 0)
    tail = [place.plane(col, order[3]) for col in range(3)]

    def send_tail(o, _):
        for col in range(3):
            send(col, tail[col], o)
        return 0
    lax.fori_loop(0, 32, send_tail, 0)
    for col in range(3):
        rb_ref[col, me] = sb_ref[col, slot_of(col, place)]
    gather.drain()
    bytes_wait(rb_ref.at[:, pl.ds(0, 127)], fsem)
    bytes_wait(rb_ref.at[:, pl.ds(0, 127)], esem)


def kernel(heads, z_ref, ws_ref, wos_ref, we_ref, woe_ref, w1_ref, w2_ref, wb_ref, bm_ref, pm_ref, um1_ref, um2_ref, y_ref,
           xc_ref, b_ref, gb1_ref, gb2_ref, rb1_ref, rb2_ref, u_ref, q_ref, g_ref, kT_ref, v_ref, bf_ref, hb_ref, sb_ref, sa_ref, sb2_ref, pa_ref, pb_ref,
           gs1, gr1, gs2, gr2, e1, f1, e2, f2):
    place = Place()
    work = (u_ref, q_ref, g_ref, kT_ref, v_ref, bf_ref, hb_ref, sb_ref, (sa_ref, sb2_ref), (pa_ref, pb_ref))
    load_rows(z_ref, xc_ref)
    stage(False, place, Gather(place, b_ref.at[0], gb1_ref, gs1, gr1), heads, xc_ref, b_ref.at[0], gb1_ref, ws_ref, wb_ref.at[0], wos_ref, w1_ref, w2_ref,
          bm_ref, pm_ref, y_ref, rb1_ref, e1, f1, *work)
    receive_rows(rb1_ref, um1_ref, xc_ref)
    stage(True, place, Gather(place, b_ref.at[1], gb2_ref, gs2, gr2), heads, xc_ref, b_ref.at[1], gb2_ref, we_ref, wb_ref.at[1], woe_ref, w1_ref, w2_ref,
          bm_ref, pm_ref, y_ref, rb2_ref, e2, f2, *work)
    finish_rows(rb2_ref, um2_ref, y_ref)


def pack_matrix():
    m = np.zeros((8, 16, 6, 2, 8), np.float32)
    for k in range(8):
        for i in range(6):
            for r in range(2):
                m[k, i * 2 + r, i, r, k] = 1
    return jnp.asarray(m.reshape(128, 96), BF16)


def unpack_matrix(swap):
    m = np.zeros((2, 6, 8, 8, 16), np.float32)
    for k in range(8):
        for i in range(6):
            for r in range(2):
                row = (k % 2) * 4 + k // 2 if swap else k
                m[r, i, row, k, i * 2 + r] = 1
    return jnp.asarray(m.reshape(96, 128), BF16)


def bias_matrix(heads):
    m = np.zeros((heads, 2, 32, 32, 2, heads), np.float32)
    for k in range(32):
        for r in range(2):
            for h in range(heads):
                m[h, r, k, k, r, h] = 1
    return jnp.asarray(m.reshape(256, 256), BF16)


def solution(mesh):
    devs = mesh.shape['sp']
    row_spec = P(('dp', 'sp'), None, None)
    vmem = pl.BlockSpec(memory_space=pltpu.VMEM)
    dma = pltpu.SemaphoreType.DMA

    def local_fn(z, wqkvg_s, wb_s, wo_s, wqkvg_e, wb_e, wo_e, w1, w2):
        per, n, c = z.shape
        heads = wb_s.shape[0]
        wb = jnp.stack([wb_s, wb_e])
        none = jnp.zeros_like(wb)
        wb = jnp.stack([jnp.concatenate([wb, none], 1), jnp.concatenate([none, wb], 1)], 1)
        args = (z, wqkvg_s, wo_s, wqkvg_e, wo_e, w1, w2, wb, bias_matrix(heads), pack_matrix(), unpack_matrix(True), unpack_matrix(False))
        return pl.pallas_call(
            functools.partial(kernel, heads), in_specs=[vmem] * len(args), out_specs=vmem,
            out_shape=jax.ShapeDtypeStruct(z.shape, F32),
            scratch_shapes=[
                pltpu.VMEM((per, n, c), F32), pltpu.VMEM((2, 3, 8, n), BF16),
                pltpu.VMEM((3, devs, 8, n), BF16), pltpu.VMEM((3, devs, 8, n), BF16),
                pltpu.VMEM((3, devs, 16, c), BF16), pltpu.VMEM((3, devs, 16, c), BF16),
                pltpu.VMEM((per, n, c), BF16), pltpu.VMEM((per, n, c), BF16), pltpu.VMEM((per, n, c), F32),
                pltpu.VMEM((per, c, n), BF16), pltpu.VMEM((per, n, 2 * c), BF16), pltpu.VMEM((heads * n // 4, n), F32),
                pltpu.VMEM((per, n // 4, c), F32), pltpu.VMEM((3, devs, 16, c), BF16),
                pltpu.VMEM((heads * n // 4, n), F32), pltpu.VMEM((heads * n // 4, n), F32),
                pltpu.VMEM((heads * n // 4, n), BF16), pltpu.VMEM((heads * n // 4, n), BF16),
                dma, dma((3, 9)), dma, dma((3, 9)), dma, dma, dma, dma],
            compiler_params=pltpu.CompilerParams(has_side_effects=True, vmem_limit_bytes=60 * 2**20), name='block')(*args)

    return jax.shard_map(local_fn, mesh=mesh, in_specs=(row_spec,) + (P(),) * 8, out_specs=row_spec, check_vma=False)
```

time: 172 us -> 147 us (0.85)
  Pallas kernels: 168 us -> 142 us
    pallas_call x1, Pallas kernels: 168 us -> 142 us  [local_fn(): pl.pallas_call(functools.partial(kernel, heads), in_specs=[vmem] * len(ar...]
where the time goes in v4:
time: 147 us; the launch traced here: 146 us
  Pallas kernels  142 us (97%)
  local copies, waits for them, and re-layouts  3.23 us (2%)
    pallas_call x1, Pallas kernels, local_fn(): pl.pallas_call(functools.partial(kernel, heads), in_specs=[vmem] * len(ar...  142 us
    unnamed x1, local copies, waits for them, and re-layouts  3.22 us

profile of v4, /device:TPU:1, one launch (start us, length us, event | category | flops | bytes accessed | tf_op | source)
XLA Modules:
  0.0 146.5 jit_solution(1819904423549298270)
XLA Ops:
  0.0 0.7 pad_maximum_fusion.1
  0.7 0.6 pad_maximum_fusion.wb_ref
  1.3 141.9 %block.1 = f32[6,768,128]{2,1,0:T(8,128)} custom-call(f32[6,768,128]{2,1,0:T(8,128)} %z_ref.1, bf16[128,512]{1,0:T(8,128)(2,1)} %ws_ref.1, bf16[128,128]{1,0:T(8,128)(2,1)} %wos_ref.1, bf16[128,512]{1,0:T(8,128)(2,1)} %we_ref.1, bf16[128,128]{1,0:T(8,128)(2,1)} %woe_ref.1, bf16[128,512]{1,0:T(8,128)(2,1)} %w1_ref.1, bf16[512,128]{1,0:T(8,128)(2,1)} %w2_ref.1, ...), custom_call_target="tpu_custom_call" | custom-call | tf_op jit(solution)/shard_map/block/pallas_call | solution.py:395
  143.3 3.2 %copy.16 = f32[6,768,128]{2,1,0:T(8,128)} copy(f32[6,768,128]{2,1,0:T(8,128)} %block.1) | data formatting | bytes 4718592
  (1 shorter events, 0.0 us)

commit v5 on v4

v5 whole, which is shorter than its diff:
```python
import functools
import math
import jax
import jax.numpy as jnp
import numpy as np
from jax import lax
from jax.experimental import pallas as pl
from jax.experimental.pallas import tpu as pltpu
from jax.sharding import PartitionSpec as P

F32, BF16 = jnp.float32, jnp.bfloat16
MESH = pl.DeviceIdType.MESH
LOG2E = math.log2(math.e)
EPS = 1e-5
X, Y, Z = 0, 1, 2
COLOURS = range(3)
PAIR = range(2)
QUAD = range(4)
HALF, SIDE, PLANE = 16, 32, 64
DEV = (2, 8, 32)
DIMS = ((X, Y, Z), (Y, Z, X), (Z, X, Y))
SLOT = ((1, 4, 32), (32, 1, 4), (4, 32, 1))


def ln(x):
    mu = jnp.mean(x, axis=-1, keepdims=True)
    c = x - mu
    var = jnp.mean(c * c, axis=-1, keepdims=True)
    return (c * lax.rsqrt(var + EPS)).astype(BF16)


def dotf(a, b):
    return jnp.dot(a, b, preferred_element_type=F32)


def dot_nt(a, b):
    return lax.dot_general(a, b, (((1,), (1,)), ((), ())), preferred_element_type=F32)


def mult(v, k):
    return pl.multiple_of(v, k)


def rcopy(src, dst, ssem, rsem, peer):
    return pltpu.make_async_remote_copy(src_ref=src, dst_ref=dst, send_sem=ssem, recv_sem=rsem, device_id={'sp': peer}, device_id_type=MESH)


def bytes_wait(ref, sem):
    pltpu.make_async_copy(ref, ref, sem).wait()


class Place:
    def __init__(self):
        self.me = lax.axis_index('sp')
        self.core = lax.rem(self.me, 2)
        self.at = [lax.rem(self.me // s, 4) for s in DEV]

    def ring(self, dim, t):
        return self.me + (lax.rem(self.at[dim] + t, 4) - self.at[dim]) * DEV[dim]

    def plane(self, c, t):
        return lax.rem(self.at[DIMS[c][2]] + t, 4)


def slot_of(c, place):
    return place.core * HALF + sum(place.at[d] * SLOT[c][d] for d in COLOURS)


def dest_of(c, plane, k):
    if c == 0:
        return plane * SIDE + lax.rem(k, HALF) * 2 + k // HALF
    if c == 1:
        return lax.rem(k, HALF) * 8 + plane * 2 + k // HALF
    return lax.rem(k, 4) * SIDE + plane * 8 + lax.rem(k // 4, 4) * 2 + k // HALF


class Gather:
    def __init__(self, place, b_ref, g_ref, ssem, rsem):
        self.p, self.b, self.g, self.ssem, self.rsem = place, b_ref, g_ref, ssem, rsem

    def push(self, c, start, count, peer, k):
        part = self.g.at[c, pl.ds(start, count)]
        rcopy(part, part, self.ssem, self.rsem.at[c, k], peer).start()

    def half(self, c, t):
        return self.p.plane(c, t) * SIDE + self.p.core * HALF

    def first(self, c):
        p = self.p
        slot = slot_of(c, p)
        for t in (1, 3, 2):
            rcopy(self.b.at[c], self.g.at[c, slot], self.ssem, self.rsem.at[c, 0], p.ring(DIMS[c][0], t)).start()
        self.g[c, slot] = self.b[c]

    def second(self, c):
        p = self.p
        b = DIMS[c][1]
        bytes_wait(self.g.at[c, pl.ds(0, 3)], self.rsem.at[c, 0])
        for t in (1, 3, 2):
            self.push(c, self.half(c, 0) + p.at[b] * 4, 4, p.ring(b, t), 1)

    def third(self, c):
        p = self.p
        d = DIMS[c][2]
        bytes_wait(self.g.at[c, pl.ds(0, 12)], self.rsem.at[c, 1])
        self.push(c, self.half(c, 0), HALF, p.me ^ 1, 5)
        self.push(c, self.half(c, 0), HALF, p.ring(d, 1), 2)
        self.push(c, self.half(c, 0), HALF, p.ring(d, 3), 3)

    def forward(self):
        p = self.p
        for side, t in ((0, 3), (1, 1)):
            for c in COLOURS:
                bytes_wait(self.g.at[c, pl.ds(0, HALF)], self.rsem.at[c, 2 + side])
                self.push(c, self.half(c, t), HALF, p.me ^ 1, 6 + side)
                self.push(c, self.half(c, t) + side * 8, 8, p.ring(DIMS[c][2], 4 - t), 4)

    def last(self):
        for c in COLOURS:
            bytes_wait(self.g.at[c, pl.ds(0, HALF)], self.rsem.at[c, 4])
            self.push(c, self.half(c, 2), HALF, self.p.me ^ 1, 8)

    def partner_wait(self, k):
        for c in COLOURS:
            bytes_wait(self.g.at[c, pl.ds(0, HALF)], self.rsem.at[c, k])

    def drain(self):
        for c in COLOURS:
            bytes_wait(self.g.at[c, pl.ds(0, 127)], self.ssem)


def load_rows(z_ref, xc_ref):
    def body(i, _):
        for r2 in PAIR:
            for p in QUAD:
                for core in PAIR:
                    at = p * PLANE + r2 * SIDE + core * HALF
                    xc_ref[i, pl.ds(at, HALF), :] = z_ref[i, pl.ds((p * SIDE + core) * 6 + r2, HALF, stride=12), :]
                    xc_ref[i, pl.ds(256 + at, HALF), :] = z_ref[i, pl.ds((p * 2 + core) * 6 + 2 + r2, HALF, stride=48), :]
                    for x in QUAD:
                        xc_ref[i, pl.ds(512 + at + x * 4, 4), :] = z_ref[i, pl.ds((p * 8 + x * 2 + core) * 6 + 4 + r2, 4, stride=192), :]
        return 0
    lax.fori_loop(0, z_ref.shape[0], body, 0)


def store_rows(place, y_ref, hb_ref, t):
    def body(i, _):
        p0, p1, p2 = (place.plane(c, t) for c in COLOURS)
        for r2 in PAIR:
            for core in PAIR:
                at = r2 * SIDE + core * HALF
                y_ref[i, pl.ds(p0 * 192 + core * 6 + r2, HALF, stride=12), :] = hb_ref[i, pl.ds(at, HALF), :]
                y_ref[i, pl.ds(p1 * 12 + core * 6 + 2 + r2, HALF, stride=48), :] = hb_ref[i, pl.ds(PLANE + at, HALF), :]
                for x in QUAD:
                    y_ref[i, pl.ds(p2 * 48 + x * 12 + core * 6 + 4 + r2, 4, stride=192), :] = hb_ref[i, pl.ds(128 + at + x * 4, 4), :]
        return 0
    lax.fori_loop(0, y_ref.shape[0], body, 0)


def inbox(c, place):
    x, y, z = place.at
    if c == 0:
        return place.me
    if c == 1:
        return x * SIDE + z * 8 + y * 2 + place.core
    return y * SIDE + z * 8 + x * 2 + place.core


def each_plane(place, rb_ref, esem, fn):
    def body(step, _):
        @pl.when(step == 0)
        def _():
            bytes_wait(rb_ref.at[:, pl.ds(0, 31)], esem.at[step])

        @pl.when(step > 0)
        def _():
            bytes_wait(rb_ref.at[:, pl.ds(0, SIDE)], esem.at[step])
        t = jnp.where(step == 1, 1, jnp.where(step == 2, 3, jnp.where(step == 3, 2, 0)))
        for c in COLOURS:
            q = place.plane(c, t)
            for g in QUAD:
                fn(c, q, g, rb_ref[c, pl.ds(mult(q * SIDE + g * 8, 8), 8)].reshape(96, 128))
        return 0
    lax.fori_loop(0, 4, body, 0)


def receive_rows(place, rb_ref, esem, um_ref, xc_ref):
    def put(c, q, g, x):
        f = dotf(um_ref[...], x)
        for b in PAIR:
            for r in range(6):
                for core in PAIR:
                    v = f[(b * 6 + r) * 8 + core * 4:(b * 6 + r) * 8 + core * 4 + 4]
                    at = (r % 2) * SIDE + core * HALF
                    if c == 1:
                        rows = (pl.ds(g * PLANE + at + q, 4, stride=4), pl.ds(mult(q * PLANE, PLANE) + 256 + at + g * 4, 4), pl.ds(512 + at + q * 4 + g, 4, stride=PLANE))
                    else:
                        zz, y = (q, g) if c == 0 else (g, q)
                        first = pl.ds(mult(q * PLANE, PLANE) + at + g * 4, 4) if c == 0 else pl.ds(g * PLANE + at + q * 4, 4)
                        rows = (first, pl.ds(256 + at + zz * 4 + y, 4, stride=PLANE), pl.ds(512 + at + y * PLANE + zz, 4, stride=4))
                    xc_ref[2 * c + b, rows[r // 2], :] = v
    each_plane(place, rb_ref, esem, put)


def finish_rows(place, rb_ref, esem, um1_ref, um2_ref, y_ref):
    def put(c, q, g, x):
        f = dotf(um1_ref[...] if c == 1 else um2_ref[...], x)
        for b in PAIR:
            for r in range(6):
                at = (b * 6 + r) * 8
                if c == 1:
                    for core in PAIR:
                        rows = pl.ds(g * 192 + q * 12 + core * 6 + r, 4, stride=48)
                        y_ref[2 * c + b, rows, :] = y_ref[2 * c + b, rows, :] + f[at + core * 4:at + core * 4 + 4]
                else:
                    rows = pl.ds((q * SIDE + g * 8) * 6 + r if c == 0 else (g * SIDE + q * 8) * 6 + r, 8, stride=6)
                    y_ref[2 * c + b, rows, :] = y_ref[2 * c + b, rows, :] + f[at:at + 8]
    each_plane(place, rb_ref, esem, put)


def stage(end, place, gather, heads, xc_ref, b_ref, gb_ref, w_ref, wb_ref, wo_ref, w1_ref, w2_ref, bm_ref, pm_ref, y_ref, rb_ref, esem, fsem,
          u_ref, q_ref, g_ref, kT_ref, v_ref, bf_ref, hb_ref, sb_ref, s_refs, p_refs, wkT_ref, entry_wait):
    per, n, c = xc_ref.shape
    hd = c // heads
    nq = n // 4
    scale = hd ** -0.5 * LOG2E
    me = place.me

    wb = wb_ref[...].astype(F32)
    none = jnp.zeros_like(wb)
    wide = [jnp.concatenate(p, axis=0).astype(BF16) for p in ((wb, none), (none, wb))]

    def bias_rows(col, _):
        acc = None
        for r2 in PAIR:
            i = col * 2 + r2
            u = ln(xc_ref[i])
            u_ref[i] = u
            t = dot_nt(wide[r2], u)
            acc = t if acc is None else acc + t
        b_ref[col] = acc.astype(BF16)
        for k in COLOURS:
            @pl.when(col == k)
            def _():
                if k == 0 and not end:
                    entry_wait()
                gather.first(k)
        return 0
    lax.fori_loop(0, 3, bias_rows, 0)

    wkT_ref[...] = w_ref[:, c:2 * c].T

    def project(i):
        u = u_ref[i]
        kT_ref[i] = dot_nt(wkT_ref[...], u).astype(BF16)
        q_ref[i] = dotf(u, w_ref[:, :c]).astype(BF16)
        vg = dotf(u, w_ref[:, 2 * c:])
        v_ref[i, :, :c] = vg[:, :c].astype(BF16)
        if not end:
            v_ref[i, :, c:] = jnp.ones((n, c), BF16)
        g_ref[i] = jax.nn.sigmoid(vg[:, c:])

    def prepare(i, _):
        project(i)
        for col in COLOURS:
            @pl.when(i == col)
            def _():
                gather.second(col)

            @pl.when(i == col + 3)
            def _():
                gather.third(col)
        return 0
    lax.fori_loop(0, per, prepare, 0)

    order = (0, 3, 1, 2)

    def pick(step):
        return jnp.where(step == 1, 3, jnp.where(step == 2, 1, jnp.where(step == 3, 2, 0)))

    def send(col, plane, o, step):
        k = lax.rem(slot_of(col, place), SIDE) ^ o
        rcopy(sb_ref.at[col, plane * SIDE + k], rb_ref.at[col, inbox(col, place)], fsem, esem.at[step], dest_of(col, plane, k)).start()

    def finish_block(t):
        if not end:
            store_rows(place, y_ref, hb_ref, t)

    def block(step, _):
        first = isinstance(step, int)
        t = 0 if first else pick(step)
        before = None if first else [place.plane(col, pick(step - 1)) for col in COLOURS]
        gather.partner_wait(5 + step)
        planes = [place.plane(col, t) for col in COLOURS]
        for col in COLOURS:
            b = gb_ref[col, pl.ds(mult(planes[col] * SIDE, SIDE), SIDE)].reshape(256, n)
            f = dotf(bm_ref[...], b) * LOG2E
            for h in range(heads):
                bf_ref[h * nq + col * PLANE:h * nq + (col + 1) * PLANE, :] = f[h * PLANE:(h + 1) * PLANE]
        rows = [pl.ds(mult(col * 256 + planes[col] * PLANE, PLANE), PLANE) for col in COLOURS]

        lane = lax.broadcasted_iota(jnp.int32, (nq, c), 1) // hd

        def scores(i):
            qb = jnp.concatenate([q_ref[i, r, :] for r in rows], axis=0)
            qm = jnp.concatenate([jnp.where(lane == h, qb, jnp.zeros_like(qb)) for h in range(heads)], axis=0)
            s_refs[i % 2][...] = dotf(qm, kT_ref[i]) * scale + bf_ref[...]

        def soften(i):
            t = s_refs[i % 2][...]
            m = jnp.max(t, axis=-1, keepdims=True)
            p_refs[i % 2][...] = jnp.exp2(t - m).astype(BF16)

        def mix(i):
            o = dotf(p_refs[i % 2][...], v_ref[i])
            o = o[:, :c] / o[:, c:]
            res = jnp.zeros((nq, c), F32)
            for h in range(heads):
                res = jnp.where(lane == h, o[h * nq:(h + 1) * nq], res)
            og = (res * jnp.concatenate([g_ref[i, r, :] for r in rows], axis=0)).astype(BF16)
            upd = dotf(og, wo_ref[...])
            if end:
                hb_ref[i] = upd
            else:
                hb_ref[i] = jnp.concatenate([xc_ref[i, r, :] for r in rows], axis=0) + upd

        if not first:
            @pl.when(step > 1)
            def _():
                for col in COLOURS:
                    send(col, before[col], 0, step - 1)
        scores(0)
        for i in range(per):
            if not first:
                for o in range(1 + i * 31 // per, 1 + (i + 1) * 31 // per):
                    for col in COLOURS:
                        send(col, before[col], o, step - 1)
            if i + 1 < per:
                scores(i + 1)
            soften(i)
            if i > 0:
                mix(i - 1)
        mix(per - 1)
        if first:
            gather.forward()
        else:
            @pl.when(step == 1)
            def _():
                gather.last()

        if end:
            def trans(i, _):
                upd = jnp.concatenate([hb_ref[2 * i], hb_ref[2 * i + 1]], axis=0)
                two = jnp.concatenate([xc_ref[2 * i + a, r, :] for a in PAIR for r in rows], axis=0) + upd
                hid = jnp.maximum(dotf(ln(two), w1_ref[...]), 0).astype(BF16)
                new = upd + dotf(hid, w2_ref[...])
                hb_ref[2 * i] = new[:nq]
                hb_ref[2 * i + 1] = new[nq:]
                return 0
            lax.fori_loop(0, per // 2, trans, 0, unroll=3)
        def pack(kg, _):
            for col in COLOURS:
                x = jnp.concatenate([hb_ref[i, pl.ds(mult(col * PLANE + r2 * SIDE + kg * 8, 8), 8), :] for i in range(per) for r2 in PAIR], axis=0)
                f = dotf(pm_ref[...], x.astype(BF16)).reshape(8, 12, c).astype(BF16)
                sb_ref[col, pl.ds(mult(planes[col] * SIDE + kg * 8, 8), 8)] = f
            return 0
        lax.fori_loop(0, 4, pack, 0, unroll=4)
        if first:
            finish_block(0)
        else:
            @pl.when(step < 3)
            def _():
                finish_block(t)

        return 0

    block(0, 0)
    lax.fori_loop(1, 4, block, 0)
    tail = [place.plane(col, order[3]) for col in COLOURS]

    def send_tail(o, _):
        for col in COLOURS:
            send(col, tail[col], o, 3)
        return 0
    lax.fori_loop(0, SIDE, send_tail, 0)
    finish_block(order[3])
    for col in COLOURS:
        rb_ref[col, inbox(col, place)] = sb_ref[col, slot_of(col, place)]


def drain(gather, rb_ref, fsem):
    gather.drain()
    bytes_wait(rb_ref.at[:, pl.ds(0, 127)], fsem)


def kernel(heads, devs, z_ref, ws_ref, wbs_ref, wos_ref, we_ref, wbe_ref, woe_ref, w1_ref, w2_ref, bm_ref, pm_ref, um1_ref, um2_ref, y_ref,
           xc_ref, b_ref, gb1_ref, gb2_ref, rb1_ref, rb2_ref, u_ref, q_ref, g_ref, kT_ref, v_ref, bf_ref, hb_ref, sb_ref, sa_ref, sb2_ref, pa_ref, pb_ref, wkT_ref,
           gs1, gr1, gs2, gr2, e1, f1, e2, f2):
    place = Place()
    barrier = pltpu.get_barrier_semaphore()

    def greet(k, _):
        pl.semaphore_signal(barrier, inc=1, device_id={'sp': place.me ^ k}, device_id_type=MESH)
        return 0
    lax.fori_loop(1, devs, greet, 0)

    def entry_wait():
        pl.semaphore_wait(barrier, devs - 1)
    work = (u_ref, q_ref, g_ref, kT_ref, v_ref, bf_ref, hb_ref, sb_ref, (sa_ref, sb2_ref), (pa_ref, pb_ref), wkT_ref, entry_wait)
    load_rows(z_ref, xc_ref)
    gather = Gather(place, b_ref.at[0], gb1_ref, gs1, gr1)
    stage(False, place, gather, heads, xc_ref, b_ref.at[0], gb1_ref, ws_ref, wbs_ref, wos_ref, w1_ref, w2_ref,
          bm_ref, pm_ref, y_ref, rb1_ref, e1, f1, *work)
    receive_rows(place, rb1_ref, e1, um1_ref, xc_ref)
    drain(gather, rb1_ref, f1)
    gather = Gather(place, b_ref.at[1], gb2_ref, gs2, gr2)
    stage(True, place, gather, heads, xc_ref, b_ref.at[1], gb2_ref, we_ref, wbe_ref, woe_ref, w1_ref, w2_ref,
          bm_ref, pm_ref, y_ref, rb2_ref, e2, f2, *work)
    finish_rows(place, rb2_ref, e2, um1_ref, um2_ref, y_ref)
    drain(gather, rb2_ref, f2)


def pack_matrix():
    m = np.zeros((8, 12, 6, 2, 8), np.float32)
    for k in range(8):
        for i in range(6):
            for r in PAIR:
                m[k, i * 2 + r, i, r, k] = 1
    return jnp.asarray(m.reshape(96, 96), BF16)


def unpack_matrix(swap):
    m = np.zeros((2, 6, 8, 8, 12), np.float32)
    for k in range(8):
        for i in range(6):
            for r in PAIR:
                row = (k % 2) * 4 + k // 2 if swap else k
                m[r, i, row, k, i * 2 + r] = 1
    return jnp.asarray(m.reshape(96, 96), BF16)


def bias_matrix(heads):
    m = np.zeros((heads, 2, SIDE, SIDE, 2, heads), np.float32)
    for k in range(SIDE):
        for r in PAIR:
            for h in range(heads):
                m[h, r, k, k, r, h] = 1
    return jnp.asarray(m.reshape(256, 256), BF16)


def solution(mesh):
    devs = mesh.shape['sp']
    row_spec = P(('dp', 'sp'), None, None)
    vmem = pl.BlockSpec(memory_space=pltpu.VMEM)
    dma = pltpu.SemaphoreType.DMA

    def local_fn(z, wqkvg_s, wb_s, wo_s, wqkvg_e, wb_e, wo_e, w1, w2):
        per, n, c = z.shape
        heads = wb_s.shape[0]
        args = (z, wqkvg_s, wb_s, wo_s, wqkvg_e, wb_e, wo_e, w1, w2, bias_matrix(heads), pack_matrix(), unpack_matrix(True), unpack_matrix(False))
        return pl.pallas_call(
            functools.partial(kernel, heads, devs), in_specs=[vmem] * len(args), out_specs=vmem,
            out_shape=jax.ShapeDtypeStruct(z.shape, F32),
            scratch_shapes=[
                pltpu.VMEM((per, n, c), F32), pltpu.VMEM((2, 3, 8, n), BF16),
                pltpu.VMEM((3, devs, 8, n), BF16), pltpu.VMEM((3, devs, 8, n), BF16),
                pltpu.VMEM((3, devs, 12, c), BF16), pltpu.VMEM((3, devs, 12, c), BF16),
                pltpu.VMEM((per, n, c), BF16), pltpu.VMEM((per, n, c), BF16), pltpu.VMEM((per, n, c), F32),
                pltpu.VMEM((per, c, n), BF16), pltpu.VMEM((per, n, 2 * c), BF16), pltpu.VMEM((heads * n // 4, n), F32),
                pltpu.VMEM((per, n // 4, c), F32), pltpu.VMEM((3, devs, 12, c), BF16),
                pltpu.VMEM((heads * n // 4, n), F32), pltpu.VMEM((heads * n // 4, n), F32),
                pltpu.VMEM((heads * n // 4, n), BF16), pltpu.VMEM((heads * n // 4, n), BF16),
                pltpu.VMEM((c, c), BF16),
                dma, dma((3, 9)), dma, dma((3, 9)), dma((4,)), dma, dma((4,)), dma],
            compiler_params=pltpu.CompilerParams(has_side_effects=True, collective_id=0, vmem_limit_bytes=60 * 2**20), name='block')(*args)

    return jax.shard_map(local_fn, mesh=mesh, in_specs=(row_spec,) + (P(),) * 8, out_specs=row_spec, check_vma=False)
```

time: 147 us -> 137 us (0.932)
  Pallas kernels: 142 us -> 133 us
    pallas_call x1, Pallas kernels: 142 us -> 133 us  [local_fn(): pl.pallas_call(functools.partial(kernel, heads, devs), in_specs=[vmem] *...]
where the time goes in v5:
time: 137 us; the launch traced here: 136 us
  Pallas kernels  133 us (97%)
  local copies, waits for them, and re-layouts  3.22 us (2%)
    pallas_call x1, Pallas kernels, local_fn(): pl.pallas_call(functools.partial(kernel, heads, devs), in_specs=[vmem] *...  133 us
    unnamed x1, local copies, waits for them, and re-layouts  3.22 us

profile of v5, /device:TPU:1, one launch (start us, length us, event | category | flops | bytes accessed | tf_op | source)
XLA Modules:
  0.0 136.4 jit_solution(2241891132278574222)
XLA Ops:
  0.0 133.2 %block.1 = f32[6,768,128]{2,1,0:T(8,128)} custom-call(f32[6,768,128]{2,1,0:T(8,128)} %z_ref.1, bf16[128,512]{1,0:T(8,128)(2,1)} %ws_ref.1, bf16[4,128]{1,0:T(4,128)(2,1)} %wbs_ref.1, bf16[128,128]{1,0:T(8,128)(2,1)} %wos_ref.1, bf16[128,512]{1,0:T(8,128)(2,1)} %we_ref.1, bf16[4,128]{1,0:T(4,128)(2,1)} %wbe_ref.1, bf16[128,128]{1,0:T(8,128)(2,1)} %woe_ref.1, ...), custom_call_target="tpu_custom_call" | custom-call | tf_op jit(solution)/shard_map/block/pallas_call | solution.py:461
  133.2 3.2 %copy.15 = f32[6,768,128]{2,1,0:T(8,128)} copy(f32[6,768,128]{2,1,0:T(8,128)} %block.1) | data formatting | bytes 4718592

commit v6 on v5

--- a/solution.py
+++ b/solution.py
@@ -112,13 +112,13 @@
         for side, t in ((0, 3), (1, 1)):
             for c in COLOURS:
                 bytes_wait(self.g.at[c, pl.ds(0, HALF)], self.rsem.at[c, 2 + side])
-                self.push(c, self.half(c, t), HALF, p.me ^ 1, 6 + side)
+                self.push(c, self.half(c, t), HALF, p.me ^ 1, 6 + 2 * side)
                 self.push(c, self.half(c, t) + side * 8, 8, p.ring(DIMS[c][2], 4 - t), 4)
 
     def last(self):
         for c in COLOURS:
             bytes_wait(self.g.at[c, pl.ds(0, HALF)], self.rsem.at[c, 4])
-            self.push(c, self.half(c, 2), HALF, self.p.me ^ 1, 8)
+            self.push(c, self.half(c, 2), HALF, self.p.me ^ 1, 7)
 
     def partner_wait(self, k):
         for c in COLOURS:
@@ -175,9 +175,8 @@
         @pl.when(step > 0)
         def _():
             bytes_wait(rb_ref.at[:, pl.ds(0, SIDE)], esem.at[step])
-        t = jnp.where(step == 1, 1, jnp.where(step == 2, 3, jnp.where(step == 3, 2, 0)))
         for c in COLOURS:
-            q = place.plane(c, t)
+            q = place.plane(c, step)
             for g in QUAD:
                 fn(c, q, g, rb_ref[c, pl.ds(mult(q * SIDE + g * 8, 8), 8)].reshape(96, 128))
         return 0
@@ -273,10 +272,10 @@
         return 0
     lax.fori_loop(0, per, prepare, 0)
 
-    order = (0, 3, 1, 2)
+    order = (0, 3, 2, 1)
 
     def pick(step):
-        return jnp.where(step == 1, 3, jnp.where(step == 2, 1, jnp.where(step == 3, 2, 0)))
+        return lax.rem(4 - step, 4)
 
     def send(col, plane, o, step):
         k = lax.rem(slot_of(col, place), SIDE) ^ o
@@ -399,13 +398,12 @@
     place = Place()
     barrier = pltpu.get_barrier_semaphore()
 
-    def greet(k, _):
-        pl.semaphore_signal(barrier, inc=1, device_id={'sp': place.me ^ k}, device_id_type=MESH)
-        return 0
-    lax.fori_loop(1, devs, greet, 0)
+    friends = [place.me ^ 1] + [place.ring(d, t) for d in COLOURS for t in QUAD if t]
+    for peer in friends:
+        pl.semaphore_signal(barrier, inc=1, device_id={'sp': peer}, device_id_type=MESH)
 
     def entry_wait():
-        pl.semaphore_wait(barrier, devs - 1)
+        pl.semaphore_wait(barrier, len(friends))
     work = (u_ref, q_ref, g_ref, kT_ref, v_ref, bf_ref, hb_ref, sb_ref, (sa_ref, sb2_ref), (pa_ref, pb_ref), wkT_ref, entry_wait)
     load_rows(z_ref, xc_ref)
     gather = Gather(place, b_ref.at[0], gb1_ref, gs1, gr1)

time: 137 us -> 136 us (level)
  no operation moved by 1% of the time
where the time goes in v6:
time: 136 us; the launch traced here: 135 us
  Pallas kernels  132 us (97%)
  local copies, waits for them, and re-layouts  3.22 us (2%)
    pallas_call x1, Pallas kernels, local_fn(): pl.pallas_call(functools.partial(kernel, heads, devs), in_specs=[vmem] *...  132 us
    unnamed x1, local copies, waits for them, and re-layouts  3.22 us

profile of v6, /device:TPU:1, one launch (start us, length us, event | category | flops | bytes accessed | tf_op | source)
XLA Modules:
  0.0 135.4 jit_solution(16836571832066665826)
XLA Ops:
  0.0 132.2 %block.1 = f32[6,768,128]{2,1,0:T(8,128)} custom-call(f32[6,768,128]{2,1,0:T(8,128)} %z_ref.1, bf16[128,512]{1,0:T(8,128)(2,1)} %ws_ref.1, bf16[4,128]{1,0:T(4,128)(2,1)} %wbs_ref.1, bf16[128,128]{1,0:T(8,128)(2,1)} %wos_ref.1, bf16[128,512]{1,0:T(8,128)(2,1)} %we_ref.1, bf16[4,128]{1,0:T(4,128)(2,1)} %wbe_ref.1, bf16[128,128]{1,0:T(8,128)(2,1)} %woe_ref.1, ...), custom_call_target="tpu_custom_call" | custom-call | tf_op jit(solution)/shard_map/block/pallas_call | solution.py:459
  132.2 3.2 %copy.15 = f32[6,768,128]{2,1,0:T(8,128)} copy(f32[6,768,128]{2,1,0:T(8,128)} %block.1) | data formatting | bytes 4718592

commit v7 on v6

--- a/solution.py
+++ b/solution.py
@@ -305,13 +305,10 @@
             qm = jnp.concatenate([jnp.where(lane == h, qb, jnp.zeros_like(qb)) for h in range(heads)], axis=0)
             s_refs[i % 2][...] = dotf(qm, kT_ref[i]) * scale + bf_ref[...]
 
-        def soften(i):
+        def mix(i):
             t = s_refs[i % 2][...]
             m = jnp.max(t, axis=-1, keepdims=True)
-            p_refs[i % 2][...] = jnp.exp2(t - m).astype(BF16)
-
-        def mix(i):
-            o = dotf(p_refs[i % 2][...], v_ref[i])
+            o = dotf(jnp.exp2(t - m).astype(BF16), v_ref[i])
             o = o[:, :c] / o[:, c:]
             res = jnp.zeros((nq, c), F32)
             for h in range(heads):
@@ -336,10 +333,7 @@
                         send(col, before[col], o, step - 1)
             if i + 1 < per:
                 scores(i + 1)
-            soften(i)
-            if i > 0:
-                mix(i - 1)
-        mix(per - 1)
+            mix(i)
         if first:
             gather.forward()
         else:

time: 136 us -> 126 us (0.926)
  Pallas kernels: 132 us -> 122 us
    pallas_call x1, Pallas kernels: 132 us -> 122 us  [local_fn(): pl.pallas_call(functools.partial(kernel, heads, devs), in_specs=[vmem] *...]
where the time goes in v7:
time: 126 us
  Pallas kernels  122 us (97%)
  local copies, waits for them, and re-layouts  3.22 us (3%)
    pallas_call x1, Pallas kernels, local_fn(): pl.pallas_call(functools.partial(kernel, heads, devs), in_specs=[vmem] *...  122 us
    unnamed x1, local copies, waits for them, and re-layouts  3.22 us

profile of v7, /device:TPU:1, one launch (start us, length us, event | category | flops | bytes accessed | tf_op | source)
XLA Modules:
  0.0 125.5 jit_solution(16493642351844910230)
XLA Ops:
  0.0 122.3 %block.1 = f32[6,768,128]{2,1,0:T(8,128)} custom-call(f32[6,768,128]{2,1,0:T(8,128)} %z_ref.1, bf16[128,512]{1,0:T(8,128)(2,1)} %ws_ref.1, bf16[4,128]{1,0:T(4,128)(2,1)} %wbs_ref.1, bf16[128,128]{1,0:T(8,128)(2,1)} %wos_ref.1, bf16[128,512]{1,0:T(8,128)(2,1)} %we_ref.1, bf16[4,128]{1,0:T(4,128)(2,1)} %wbe_ref.1, bf16[128,128]{1,0:T(8,128)(2,1)} %woe_ref.1, ...), custom_call_target="tpu_custom_call" | custom-call | tf_op jit(solution)/shard_map/block/pallas_call | solution.py:453
  122.3 3.2 %copy.15 = f32[6,768,128]{2,1,0:T(8,128)} copy(f32[6,768,128]{2,1,0:T(8,128)} %block.1) | data formatting | bytes 4718592

commit v8 on v7

--- a/solution.py
+++ b/solution.py
@@ -166,24 +166,34 @@
     return y * SIDE + z * 8 + x * 2 + place.core
 
 
-def each_plane(place, rb_ref, esem, fn):
+def take_plane(place, rb_ref, c, step, fn):
+    q = place.plane(c, step)
+    for g in QUAD:
+        fn(c, q, g, rb_ref[c, pl.ds(mult(q * SIDE + g * 8, 8), 8)].reshape(96, 128))
+
+
+def early_planes(place, rb_ref, esem, fn):
     def body(step, _):
-        @pl.when(step == 0)
-        def _():
-            bytes_wait(rb_ref.at[:, pl.ds(0, 31)], esem.at[step])
-
-        @pl.when(step > 0)
-        def _():
-            bytes_wait(rb_ref.at[:, pl.ds(0, SIDE)], esem.at[step])
         for c in COLOURS:
-            q = place.plane(c, step)
-            for g in QUAD:
-                fn(c, q, g, rb_ref[c, pl.ds(mult(q * SIDE + g * 8, 8), 8)].reshape(96, 128))
-        return 0
-    lax.fori_loop(0, 4, body, 0)
-
-
-def receive_rows(place, rb_ref, esem, um_ref, xc_ref):
+            @pl.when(step == 0)
+            def _():
+                bytes_wait(rb_ref.at[c, pl.ds(0, SIDE - 1)], esem.at[step, c])
+
+            @pl.when(step > 0)
+            def _():
+                bytes_wait(rb_ref.at[c, pl.ds(0, SIDE)], esem.at[step, c])
+        for c in COLOURS:
+            take_plane(place, rb_ref, c, step, fn)
+        return 0
+    lax.fori_loop(0, 3, body, 0)
+
+
+def last_plane(place, rb_ref, esem, c, fn):
+    bytes_wait(rb_ref.at[c, pl.ds(0, SIDE)], esem.at[3, c])
+    take_plane(place, rb_ref, c, 3, fn)
+
+
+def receiver(um_ref, xc_ref):
     def put(c, q, g, x):
         f = dotf(um_ref[...], x)
         for b in PAIR:
@@ -198,10 +208,10 @@
                         first = pl.ds(mult(q * PLANE, PLANE) + at + g * 4, 4) if c == 0 else pl.ds(g * PLANE + at + q * 4, 4)
                         rows = (first, pl.ds(256 + at + zz * 4 + y, 4, stride=PLANE), pl.ds(512 + at + y * PLANE + zz, 4, stride=4))
                     xc_ref[2 * c + b, rows[r // 2], :] = v
-    each_plane(place, rb_ref, esem, put)
-
-
-def finish_rows(place, rb_ref, esem, um1_ref, um2_ref, y_ref):
+    return put
+
+
+def finisher(um1_ref, um2_ref, y_ref):
     def put(c, q, g, x):
         f = dotf(um1_ref[...] if c == 1 else um2_ref[...], x)
         for b in PAIR:
@@ -214,11 +224,11 @@
                 else:
                     rows = pl.ds((q * SIDE + g * 8) * 6 + r if c == 0 else (g * SIDE + q * 8) * 6 + r, 8, stride=6)
                     y_ref[2 * c + b, rows, :] = y_ref[2 * c + b, rows, :] + f[at:at + 8]
-    each_plane(place, rb_ref, esem, put)
+    return put
 
 
 def stage(end, place, gather, heads, xc_ref, b_ref, gb_ref, w_ref, wb_ref, wo_ref, w1_ref, w2_ref, bm_ref, pm_ref, y_ref, rb_ref, esem, fsem,
-          u_ref, q_ref, g_ref, kT_ref, v_ref, bf_ref, hb_ref, sb_ref, s_refs, p_refs, wkT_ref, entry_wait):
+          u_ref, q_ref, g_ref, kT_ref, v_ref, bf_ref, hb_ref, sb_ref, s_refs, p_refs, wkT_ref, entry_wait, arrive, settle):
     per, n, c = xc_ref.shape
     hd = c // heads
     nq = n // 4
@@ -230,6 +240,10 @@
     wide = [jnp.concatenate(p, axis=0).astype(BF16) for p in ((wb, none), (none, wb))]
 
     def bias_rows(col, _):
+        for k in COLOURS:
+            @pl.when(col == k)
+            def _():
+                arrive(k)
         acc = None
         for r2 in PAIR:
             i = col * 2 + r2
@@ -272,6 +286,7 @@
         return 0
     lax.fori_loop(0, per, prepare, 0)
 
+    settle()
     order = (0, 3, 2, 1)
 
     def pick(step):
@@ -279,7 +294,7 @@
 
     def send(col, plane, o, step):
         k = lax.rem(slot_of(col, place), SIDE) ^ o
-        rcopy(sb_ref.at[col, plane * SIDE + k], rb_ref.at[col, inbox(col, place)], fsem, esem.at[step], dest_of(col, plane, k)).start()
+        rcopy(sb_ref.at[col, plane * SIDE + k], rb_ref.at[col, inbox(col, place)], fsem, esem.at[step, col], dest_of(col, plane, k)).start()
 
     def finish_block(t):
         if not end:
@@ -371,11 +386,11 @@
     lax.fori_loop(1, 4, block, 0)
     tail = [place.plane(col, order[3]) for col in COLOURS]
 
-    def send_tail(o, _):
-        for col in COLOURS:
+    for col in COLOURS:
+        def send_tail(o, _):
             send(col, tail[col], o, 3)
-        return 0
-    lax.fori_loop(0, SIDE, send_tail, 0)
+            return 0
+        lax.fori_loop(0, SIDE, send_tail, 0)
     finish_block(order[3])
     for col in COLOURS:
         rb_ref[col, inbox(col, place)] = sb_ref[col, slot_of(col, place)]
@@ -401,15 +416,20 @@
     work = (u_ref, q_ref, g_ref, kT_ref, v_ref, bf_ref, hb_ref, sb_ref, (sa_ref, sb2_ref), (pa_ref, pb_ref), wkT_ref, entry_wait)
     load_rows(z_ref, xc_ref)
     gather = Gather(place, b_ref.at[0], gb1_ref, gs1, gr1)
+    nothing = lambda *_: None
     stage(False, place, gather, heads, xc_ref, b_ref.at[0], gb1_ref, ws_ref, wbs_ref, wos_ref, w1_ref, w2_ref,
-          bm_ref, pm_ref, y_ref, rb1_ref, e1, f1, *work)
-    receive_rows(place, rb1_ref, e1, um1_ref, xc_ref)
-    drain(gather, rb1_ref, f1)
-    gather = Gather(place, b_ref.at[1], gb2_ref, gs2, gr2)
-    stage(True, place, gather, heads, xc_ref, b_ref.at[1], gb2_ref, we_ref, wbe_ref, woe_ref, w1_ref, w2_ref,
-          bm_ref, pm_ref, y_ref, rb2_ref, e2, f2, *work)
-    finish_rows(place, rb2_ref, e2, um1_ref, um2_ref, y_ref)
-    drain(gather, rb2_ref, f2)
+          bm_ref, pm_ref, y_ref, rb1_ref, e1, f1, *work, nothing, nothing)
+    put = receiver(um1_ref, xc_ref)
+    early_planes(place, rb1_ref, e1, put)
+    gather2 = Gather(place, b_ref.at[1], gb2_ref, gs2, gr2)
+    stage(True, place, gather2, heads, xc_ref, b_ref.at[1], gb2_ref, we_ref, wbe_ref, woe_ref, w1_ref, w2_ref,
+          bm_ref, pm_ref, y_ref, rb2_ref, e2, f2, *work,
+          lambda c: last_plane(place, rb1_ref, e1, c, put), lambda: drain(gather, rb1_ref, f1))
+    put2 = finisher(um1_ref, um2_ref, y_ref)
+    early_planes(place, rb2_ref, e2, put2)
+    for c in COLOURS:
+        last_plane(place, rb2_ref, e2, c, put2)
+    drain(gather2, rb2_ref, f2)
 
 
 def pack_matrix():
@@ -463,7 +483,7 @@
                 pltpu.VMEM((heads * n // 4, n), F32), pltpu.VMEM((heads * n // 4, n), F32),
                 pltpu.VMEM((heads * n // 4, n), BF16), pltpu.VMEM((heads * n // 4, n), BF16),
                 pltpu.VMEM((c, c), BF16),
-                dma, dma((3, 9)), dma, dma((3, 9)), dma((4,)), dma, dma((4,)), dma],
+                dma, dma((3, 9)), dma, dma((3, 9)), dma((4, 3)), dma, dma((4, 3)), dma],
             compiler_params=pltpu.CompilerParams(has_side_effects=True, collective_id=0, vmem_limit_bytes=60 * 2**20), name='block')(*args)
 
     return jax.shard_map(local_fn, mesh=mesh, in_specs=(row_spec,) + (P(),) * 8, out_specs=row_spec, check_vma=False)

time: 126 us -> 126 us (level)
  no operation moved by 1% of the time
where the time goes in v8:
time: 126 us
  Pallas kernels  122 us (97%)
  local copies, waits for them, and re-layouts  3.22 us (3%)
    pallas_call x1, Pallas kernels, local_fn(): pl.pallas_call(functools.partial(kernel, heads, devs), in_specs=[vmem] *...  122 us
    unnamed x1, local copies, waits for them, and re-layouts  3.22 us

profile of v8, /device:TPU:1, one launch (start us, length us, event | category | flops | bytes accessed | tf_op | source)
XLA Modules:
  0.0 125.6 jit_solution(1274948396410755609)
XLA Ops:
  0.0 122.4 %block.1 = f32[6,768,128]{2,1,0:T(8,128)} custom-call(f32[6,768,128]{2,1,0:T(8,128)} %z_ref.1, bf16[128,512]{1,0:T(8,128)(2,1)} %ws_ref.1, bf16[4,128]{1,0:T(4,128)(2,1)} %wbs_ref.1, bf16[128,128]{1,0:T(8,128)(2,1)} %wos_ref.1, bf16[128,512]{1,0:T(8,128)(2,1)} %we_ref.1, bf16[4,128]{1,0:T(4,128)(2,1)} %wbe_ref.1, bf16[128,128]{1,0:T(8,128)(2,1)} %woe_ref.1, ...), custom_call_target="tpu_custom_call" | custom-call | tf_op jit(solution)/shard_map/block/pallas_call | solution.py:473
  122.4 3.2 %copy.15 = f32[6,768,128]{2,1,0:T(8,128)} copy(f32[6,768,128]{2,1,0:T(8,128)} %block.1) | data formatting | bytes 4718592
